TPU v7x, 32 devices: a whole 2x2x4 slice. The times are simulated.
32 devices in a mesh: row: 4 (over y, x), col: 8 (over z, core).
Axes of the slice: x: 2, y: 2, z: 4, core: 2. Of those that a mesh axis runs over, the one named last changes fastest.
Arguments:
- pair: float32 [256, 256, 128], P('row', 'col'), may hold values from -6 to 6
- valid_length: int32 [1], replicated, may hold values from 64 to 255
- tri_in: bfloat16 [128, 512], replicated, may hold values from -0.5 to 0.5
- tri_gate: bfloat16 [128, 128], replicated, may hold values from -0.5 to 0.5
- tri_out: bfloat16 [128, 128], replicated, may hold values from -0.5 to 0.5
- att_in: bfloat16 [128, 512], replicated, may hold values from -16.9705627 to 16.9705627
- att_bias: bfloat16 [128, 4], replicated, may hold values from -0.5 to 0.5
- att_out: bfloat16 [128, 128], replicated, may hold values from -0.5 to 0.5
Outputs:
- pair_out: float32 [256, 256, 128], P('row', 'col')
Inputs may be any that keep to these rules, and one draw needn't show every extreme that they name: Tokens at positions below valid_length[0] are real, the rest are padding.
All inputs are finite; a program needn't handle non-finite values.
Results may differ from a plain program's by a relative error of at most 0.025.
Values may be sent and summed in bfloat16 or wider, within the bound.
No kernel may reach another device: no remote copies, remote signals or barrier semaphores. Data moves between devices by JAX's collectives and lax.ppermute only.
A program may use at most 128 MiB of HBM per device.

v0:
```python
import jax
import jax.numpy as jnp
from jax import lax
from jax.sharding import PartitionSpec as P


def layer_norm(values):
    center = values - jnp.mean(values, axis=-1, keepdims=True)
    return center * lax.rsqrt(jnp.mean(center * center, axis=-1, keepdims=True) + 1e-05)


def fold_keys(carry, keys_piece, values_piece, query_blocks, bias_heads, mask_bias):
    count = keys_piece.shape[1]
    nblocks, brows, cols_dev, heads, head_size = query_blocks.shape
    key_blocks = keys_piece.reshape(nblocks, brows, count, heads, head_size)
    value_blocks = values_piece.reshape(nblocks, brows, count, heads, head_size)

    def one_block(packed):
        query, keys, values, run_max, run_sum, accum = packed
        scores = jnp.einsum("ijhd,ikhd->ihjk", query, keys, preferred_element_type=jnp.float32)
        scores = scores + bias_heads[None] + mask_bias[None, None, None, :]
        new_max = jnp.maximum(run_max, jnp.max(scores, axis=-1))
        factor = jnp.exp(run_max - new_max)
        expo = jnp.exp(scores - new_max[..., None])
        new_sum = run_sum * factor + jnp.sum(expo, axis=-1)
        new_acc = accum * jnp.transpose(factor, (0, 2, 1))[..., None]
        new_acc = new_acc + jnp.einsum("ihjk,ikhd->ijhd", expo, values.astype(jnp.float32))
        return (new_max, new_sum, new_acc)

    return lax.map(one_block, (query_blocks, key_blocks, value_blocks) + tuple(carry))


def per_device(pair, valid_length, tri_in, tri_gate, tri_out, att_in, att_bias, att_out):
    rows_dev, cols_dev, width = pair.shape
    hidden = tri_out.shape[0]
    heads = att_bias.shape[1]
    head_size = width // heads
    total = cols_dev * lax.axis_size("col")
    row_start = lax.axis_index("row") * rows_dev
    col_start = lax.axis_index("col") * cols_dev
    tokens = jnp.arange(total)
    keep_all = (tokens < valid_length[0]).astype(jnp.float32)
    keep_rows = lax.dynamic_slice_in_dim(keep_all, row_start, rows_dev)
    keep_cols = lax.dynamic_slice_in_dim(keep_all, col_start, cols_dev)
    normed_pair = layer_norm(pair).astype(jnp.bfloat16)
    projected = jnp.dot(normed_pair, tri_in, preferred_element_type=jnp.float32)
    weight = (keep_rows[:, None] * keep_cols[None, :])[:, :, None]
    left_edges = (
        jax.nn.sigmoid(projected[..., :hidden]) * projected[..., hidden : 2 * hidden] * weight
    ).astype(jnp.bfloat16)
    right_edges = (
        jax.nn.sigmoid(projected[..., 2 * hidden : 3 * hidden])
        * projected[..., 3 * hidden :]
        * weight
    ).astype(jnp.bfloat16)
    right_rows = lax.all_gather(right_edges, "row", axis=0, tiled=True)
    swapped = lax.psum_scatter(
        jnp.einsum(
            "jkc,ikc->jic", right_rows, left_edges, preferred_element_type=jnp.float32
        ).astype(jnp.bfloat16),
        "col",
        scatter_dimension=0,
        tiled=True,
    ).astype(jnp.float32)
    normed_swapped = layer_norm(swapped).astype(jnp.bfloat16)
    tri_part = jnp.einsum(
        "jic,cd->ijd", normed_swapped, tri_out, preferred_element_type=jnp.float32
    )
    middle = (
        pair
        + jax.nn.sigmoid(jnp.dot(normed_pair, tri_gate, preferred_element_type=jnp.float32))
        * tri_part
    )
    normed_mid = layer_norm(middle).astype(jnp.bfloat16)
    bias_local = jnp.dot(normed_mid, att_bias, preferred_element_type=jnp.float32).astype(
        jnp.bfloat16
    )
    bias_rows = lax.all_gather(bias_local, "row", axis=0, tiled=True)
    bias_cols = lax.all_to_all(bias_rows, "col", split_axis=0, concat_axis=1, tiled=True)
    bias_heads = jnp.transpose(bias_cols.astype(jnp.float32), (2, 0, 1))
    mask_bias = jnp.where(tokens < valid_length[0], 0.0, -1000000000.0).astype(jnp.float32)
    nblocks = rows_dev // 8
    query = (
        jnp.dot(normed_mid, att_in[:, :width], preferred_element_type=jnp.float32)
        * head_size ** (-0.5)
    ).astype(jnp.bfloat16)
    query_blocks = query.reshape(nblocks, 8, cols_dev, heads, head_size)
    gate = jax.nn.sigmoid(
        jnp.dot(normed_mid, att_in[:, 3 * width :], preferred_element_type=jnp.float32)
    )
    start_state = (
        jnp.full((nblocks, 8, heads, cols_dev), -1e30, jnp.float32),
        jnp.zeros((nblocks, 8, heads, cols_dev), jnp.float32),
        jnp.zeros((nblocks, 8, cols_dev, heads, head_size), jnp.float32),
    )
    made = jnp.dot(
        lax.all_gather(normed_mid, "col", axis=1, tiled=True),
        att_in[:, width : 3 * width],
        preferred_element_type=jnp.float32,
    )
    keys_piece = made[..., :width].astype(jnp.bfloat16)
    values_piece = made[..., width:].astype(jnp.bfloat16)
    state = fold_keys(start_state, keys_piece, values_piece, query_blocks, bias_heads, mask_bias)
    run_sum = state[1]
    accum = state[2]
    attended = accum / jnp.transpose(run_sum, (0, 1, 3, 2))[..., None]
    attended = attended.reshape(rows_dev, cols_dev, width)
    gated = (gate * attended).astype(jnp.bfloat16)
    return middle + jnp.dot(gated, att_out, preferred_element_type=jnp.float32)


def solution(mesh):
    placed = (P("row", "col", None), P(), P(), P(), P(), P(), P(), P())
    return jax.shard_map(
        per_device, mesh=mesh, in_specs=placed, out_specs=P("row", "col", None), check_vma=False
    )
```

profile of v0, /device:TPU:0, one launch (start us, length us, event | category | flops | bytes accessed | tf_op | source)
XLA Modules:
  0.0 237.1 jit_solution(12051169796513153194)
XLA Ops:
  7.4 1.6 reduce_sum.65
  9.0 1.9 multiply_reduce_fusion.1
  10.9 2.1 fusion.40
  13.0 1.4 fusion.31
  14.5 1.7 copy.17
  16.2 36.3 %all-gather.3.cloned.1.call-done = bf16[256,32,128]{2,1,0:T(8,128)(2,1)} async-done(((bf16[64,32,128]{2,1,0:T(8,128)(2,1)}), bf16[256,32,128]{2,1,0:T(8,128)(2,1)}) %all-gather.3.cloned.1.call-update) | async-done | bytes 2097168 | tf_op jit(solution)/shard_map/all_gather | solution.py:56
  52.5 3.9 %copy.18 = bf16[256,32,128]{0,1,2:T(8,128)(2,1)S(1)} copy(bf16[256,32,128]{2,1,0:T(8,128)(2,1)} %all-gather.3.cloned.1.call-done) | data formatting | bytes 4194304 | tf_op jit(solution)/shard_map/all_gather | solution.py:56
  56.4 3.3 %convert_bitcast_fusion = bf16[256,64,128]{0,1,2:T(8,128)(2,1)} fusion(bf16[64,32,128]{0,1,2:T(8,128)(2,1)S(1)} %copy.17, bf16[256,32,128]{0,1,2:T(8,128)(2,1)S(1)} %copy.18), kind=kOutput, calls=%fused_computation.24 | convolution fusion | flops 136314880 | bytes 6815744 | tf_op jit(solution)/shard_map/jkc,ikc->jic/dot_general | solution.py:58
  59.7 7.4 %copy.19 = bf16[256,64,128]{2,1,0:T(8,128)(2,1)} copy(bf16[256,64,128]{0,1,2:T(8,128)(2,1)} %convert_bitcast_fusion) | data formatting | bytes 8388608 | tf_op jit(solution)/shard_map/convert_element_type | solution.py:60
  67.1 50.0 %reduce-scatter.2.cloned.1.call-done = bf16[32,64,128]{2,1,0:T(8,128)(2,1)} async-done(((bf16[256,64,128]{2,1,0:T(8,128)(2,1)}), bf16[32,64,128]{2,1,0:T(8,128)(2,1)}) %reduce-scatter.2.cloned.1.call-update) | async-done | bytes 524304 | tf_op jit(solution)/shard_map/reduce_scatter | solution.py:57
  117.1 1.4 convert_reduce_fusion
  118.5 1.7 fusion.28
  120.2 1.6 fusion.29
  122.4 1.7 fusion.63
  124.1 0.6 multiply_reduce_fusion
  124.8 1.4 multiply_convert_fusion
  126.2 1.8 convolution_convert_fusion.1
  128.1 9.1 %all_gather.11 = bf16[256,32,4]{1,2,0:T(4,128)(2,1)S(1)} all-gather(bf16[64,32,4]{1,2,0:T(4,128)(2,1)S(1)} %convolution_convert_fusion.1), channel_id=1, replica_groups=mesh['row'=4,'col'=8] {'row'}, dimensions={0}, use_global_device_ids=true | all-gather | bytes 81920 | tf_op jit(solution)/shard_map/all_gather | solution.py:78
  137.2 0.9 reshape.132
  138.1 3.5 %all-to-all-start = ((bf16[8,2,2048]{2,1,0:T(2,128)(2,1)}), bf16[8,2,2048]{2,1,0:T(2,128)(2,1)S(1)}, u32[]{:S(2)}, u32[]{:S(2)}) async-start(bf16[8,2,2048]{2,1,0:T(2,128)(2,1)} %reshape.132), calls=%async_computation.1 | async-start | bytes 131072 | tf_op jit(solution)/shard_map/all_to_all | solution.py:79
  141.6 2.1 fusion.25
  143.7 3.1 %reshape.116 = bf16[8,8,32,4,32]{4,3,2,1,0:T(4,128)(2,1)S(1)} reshape(bf16[64,32,128]{2,1,0:T(8,128)(2,1)} %fusion.25) | data formatting | bytes 1048576 | tf_op jit(solution)/shard_map/reshape | solution.py:87
  146.9 2.2 all-to-all-done
  149.1 0.9 reshape.133
  150.0 1.0 convert_bitcast_fusion.1
  151.0 1.1 copy.22
  152.1 1.2 reshape.121
  153.3 19.8 %all-gather.5.cloned.1.call-done = bf16[64,256,128]{2,1,0:T(8,128)(2,1)} async-done(((bf16[64,32,128]{2,1,0:T(8,128)(2,1)}), bf16[64,256,128]{2,1,0:T(8,128)(2,1)}) %all-gather.5.cloned.1.call-update) | async-done | bytes 4194320 | tf_op jit(solution)/shard_map/all_gather | solution.py:97
  173.1 4.6 %convolution_convert_fusion = bf16[64,256,256]{1,2,0:T(8,128)(2,1)S(1)} fusion(bf16[64,256,128]{2,1,0:T(8,128)(2,1)} %all-gather.5.cloned.1.call-done, bf16[128,512]{1,0:T(8,128)(2,1)} %param.15), kind=kOutput, calls=%fused_computation.23 | convolution fusion | flops 1077936128 | bytes 12648448 | tf_op jit(solution)/shard_map/dot_general | solution.py:96
  177.7 3.5 %fusion.62 = (bf16[64,256,128]{1,2,0:T(8,128)(2,1)}, bf16[64,256,128]{1,2,0:T(8,128)(2,1)}) fusion(bf16[64,256,256]{1,2,0:T(8,128)(2,1)S(1)} %convolution_convert_fusion), kind=kLoop, calls=%fused_computation.96 | loop fusion | bytes 16777216 | tf_op jit(solution)/shard_map/slice | solution.py:102
  181.2 39.1 %while.13 = (s32[]{:T(128)}, f32[8,8,4,32]{3,2,1,0:T(4,128)S(1)}, f32[8,8,32,4,32]{2,4,3,1,0:T(8,128)}, bf16[8,8,32,4,32]{4,3,2,1,0:T(4,128)(2,1)S(1)}, bf16[8,8...) while((s32[]{:T(128)}, f32[8,8,4,32]{3,2,1,0:T(4,128)S(1)}, ...), condition=%wide.region_10.11_spmd.clone, body=%wide.region_7.10_spmd.clone.sunk | while | flops 35165696 | bytes 5131381 | solution.py:30
  181.2 0.6 compare_select_fusion.2
  182.0 1.4 fusion.76
  183.4 0.4 fusion.78
  183.8 2.3 fusion.79
  186.1 0.6 compare_select_fusion.2
  186.9 1.4 fusion.76
  188.3 0.4 fusion.78
  188.8 2.3 fusion.79
  191.1 0.6 compare_select_fusion.2
  191.8 1.4 fusion.76
  193.3 0.4 fusion.78
  193.7 2.2 fusion.79
  195.9 0.6 compare_select_fusion.2
  196.7 1.4 fusion.76
  198.1 0.4 fusion.78
  198.6 2.2 fusion.79
  200.8 0.6 compare_select_fusion.2
  201.5 1.4 fusion.76
  203.0 0.4 fusion.78
  203.4 2.2 fusion.79
  205.7 0.6 compare_select_fusion.2
  206.5 1.4 fusion.76
  208.3 2.2 fusion.79
  210.6 0.6 compare_select_fusion.2
  211.3 1.4 fusion.76
  212.8 0.4 fusion.78
  213.2 2.2 fusion.79
  215.4 0.6 compare_select_fusion.2
  216.2 1.4 fusion.76
  218.1 2.2 fusion.79
  220.3 5.0 %broadcast_divide_fusion = f32[8,8,32,4,32]{2,4,3,1,0:T(8,128)} fusion(f32[8,8,32,4,32]{2,4,3,1,0:T(8,128)} %get-tuple-element.48, f32[8,8,32,4]{2,3,1,0:T(4,128)S(1)} %bitcast.104), kind=kLoop, calls=%fused_computation.25 | loop fusion | flops 262144 | bytes 2129920 | tf_op jit(solution)/shard_map/div | solution.py:106
  225.4 2.9 %copy.27 = f32[64,32,128]{2,1,0:T(8,128)S(1)} copy(f32[64,32,128]{1,2,0:T(8,128)} %bitcast.98) | data formatting | bytes 2097152 | tf_op jit(solution)/shard_map/reshape | solution.py:107
  228.2 2.3 convolution_add_fusion.1
  (59 shorter events, 2.9 us)
Async XLA Ops:
  6.5 4.4 %copy-start = (bf16[128,512]{1,0:T(8,128)(2,1)S(1)}, bf16[128,512]{1,0:T(8,128)(2,1)}, u32[]{:S(2)}) copy-start(bf16[128,512]{1,0:T(8,128)(2,1)} %param.12) | copy-start | bytes 393220
  6.5 45.9 %all-gather.3.cloned.1.call-start = ((), (), s32[]{:S(2)}) async-start(), calls=%async_computation.2 | async-start | bytes 2621440 | tf_op jit(solution)/shard_map/all_gather | solution.py:56
  14.4 102.7 %reduce-scatter.2.cloned.1.call-start = ((), (), s32[]{:S(2)}) async-start(), calls=%async_computation.3 | async-start | bytes 4718592 | tf_op jit(solution)/shard_map/reduce_scatter | solution.py:57
  67.1 54.9 %copy-start.3 = (bf16[128,128]{1,0:T(8,128)(2,1)S(1)}, bf16[128,128]{1,0:T(8,128)(2,1)}, u32[]{:S(2)}) copy-start(bf16[128,128]{1,0:T(8,128)(2,1)} %param.14) | copy-start | bytes 98308
  67.1 55.3 %copy-start.1 = (f32[64,32,128]{2,1,0:T(8,128)S(1)}, f32[64,32,128]{2,1,0:T(8,128)}, u32[]{:S(2)}) copy-start(f32[64,32,128]{2,1,0:T(8,128)} %param.10) | copy-start | bytes 3145732
  67.1 55.3 %copy-start.5 = (bf16[128,128]{1,0:T(8,128)(2,1)S(1)}, bf16[128,128]{1,0:T(8,128)(2,1)}, u32[]{:S(2)}) copy-start(bf16[128,128]{1,0:T(8,128)(2,1)} %param.13) | copy-start | bytes 98308
  67.1 106.0 %all-gather.5.cloned.1.call-start = ((), (), s32[]{:S(2)}) async-start(), calls=%async_computation.4 | async-start | bytes 4718592 | tf_op jit(solution)/shard_map/all_gather | solution.py:97
  122.3 3.9 %copy-start.4 = (bf16[128,4]{0,1:T(4,128)(2,1)S(1)}, bf16[128,4]{0,1:T(4,128)(2,1)}, u32[]{:S(2)}) copy-start(bf16[128,4]{0,1:T(4,128)(2,1)} %param.16) | copy-start | bytes 3076
  138.1 11.0 %all-to-all-start = ((bf16[8,2,2048]{2,1,0:T(2,128)(2,1)}), bf16[8,2,2048]{2,1,0:T(2,128)(2,1)S(1)}, u32[]{:S(2)}, u32[]{:S(2)}) async-start(bf16[8,2,2048]{2,1,0:T(2,128)(2,1)} %reshape.132), calls=%async_computation.1 | async-start | bytes 131072 | tf_op jit(solution)/shard_map/all_to_all | solution.py:79
  225.4 2.9 %copy-start.2 = (bf16[64,32,128]{2,1,0:T(8,128)(2,1)S(1)}, bf16[64,32,128]{2,1,0:T(8,128)(2,1)}, u32[]{:S(2)}) copy-start(bf16[64,32,128]{2,1,0:T(8,128)(2,1)} %multiply_convert_fusion) | copy-start | bytes 1572868
  225.4 2.9 %copy-start.6 = (bf16[128,128]{1,0:T(8,128)(2,1)S(1)}, bf16[128,128]{1,0:T(8,128)(2,1)}, u32[]{:S(2)}) copy-start(bf16[128,128]{1,0:T(8,128)(2,1)} %param.17) | copy-start | bytes 98308
Sparse Core Ops, SparseCore 0:
  14.5 37.8 all-gather.2
  67.2 49.8 reduce-scatter.1
  126.3 46.7 all-gather.4
where the time goes:
time: 239 us; the launch traced here: 237 us
  waiting for transfers between devices  108 us (45%)
  matrix products  47.5 us (20%)
  local copies, waits for them, and re-layouts  27.6 us (12%)
  other arithmetic  26.6 us (11%)
  between operations  14 us (6%)
  blocking collectives  9.12 us (4%)
  starting transfers between devices  3.61 us (2%)
    reduce_scatter x1, waiting for transfers between devices, per_device(): lax.psum_scatter(jnp.einsum('jkc,ikc->jic', right_rows, left_edges, prefe...  50 us
    all_gather x1, waiting for transfers between devices, per_device(): right_rows = lax.all_gather(right_edges, 'row', axis=0, tiled=True)  36.3 us
    all_gather x1, waiting for transfers between devices, per_device(): lax.all_gather(normed_mid, 'col', axis=1, tiled=True)  19.8 us
    dot_general x8, matrix products, one_block(): jnp.einsum('ihjk,ikhd->ijhd', expo, values.astype(jnp.float32))  17.9 us
    dot_general x8, matrix products, one_block(): jnp.einsum('ijhd,ikhd->ihjk', query, keys, preferred_element_type=jnp.flo...  11.3 us
    all_gather x1, blocking collectives, per_device(): bias_rows = lax.all_gather(bias_local, 'row', axis=0, tiled=True)  9.12 us
    convert_element_type x1, local copies, waits for them, and re-layouts, per_device(): swapped = lax.psum_scatter(jnp.einsum('jkc,ikc->jic', right_rows, left_ed...  7.38 us
    select_n x8, other arithmetic, per_device(): jnp.where(tokens < valid_length[0], 0.0, -1000000000.0).astype(jnp.float32)  5.17 us
  transfers between devices with their start and end apart: 4, of which 4 were waited for; matrix products, arithmetic and copies ran while one was open for 6% of the time, Pallas kernels for 0%

commit v1 on v0

v1 whole, which is shorter than its diff:
```python
import functools
import math

import jax
import jax.numpy as jnp
from jax import lax
from jax.experimental import pallas as pl
from jax.experimental.pallas import tpu as pltpu
from jax.sharding import PartitionSpec as P

BF = jnp.bfloat16
F32 = jnp.float32
LOG2E = 1.4426950408889634
NT = (((1,), (1,)), ((), ()))
TN = (((0,), (0,)), ((), ()))
NN = (((1,), (0,)), ((), ()))


def mm(a, b, dims):
    return lax.dot_general(a, b, dims, preferred_element_type=F32)


def sigmoid(v):
    return 0.5 * jnp.tanh(0.5 * v) + 0.5


def layer_norm(v, axis=-1):
    center = v - jnp.mean(v, axis=axis, keepdims=True)
    return center * lax.rsqrt(jnp.mean(center * center, axis=axis, keepdims=True) + 1e-05)


def edges_kernel(valid_ref, start_ref, x_ref, w_ref, out_ref, acc_ref):
    blocks, own, cols, width = x_ref.shape
    total = blocks * cols
    half = w_ref.shape[0] // 2
    keep_k = (lax.broadcasted_iota(jnp.int32, (1, total), 1) < valid_ref[0]).astype(F32)

    for i in range(own):
        x = x_ref[:, i].reshape(total, width).astype(F32)
        normed = layer_norm(x).astype(BF)
        keep_i = jnp.where(start_ref[0] + i < valid_ref[0], 1.0, 0.0).astype(F32)
        weight = keep_k * keep_i
        proj = mm(w_ref[...], normed, NT)
        edge = sigmoid(proj[:half]) * proj[half:] * weight
        for t in range(total // 128):
            acc_ref[t, pl.ds(i, half, stride=own), :] = edge[:, t * 128 : (t + 1) * 128]
    for t in range(total // 128):
        out_ref[:, t * 128 : (t + 1) * 128] = acc_ref[t].astype(BF)


def product_kernel(e_ref, out_ref):
    count, _, _, own, total = e_ref.shape
    left = e_ref[:, 0, 0].astype(F32).reshape(count * own, total).astype(BF)
    right = e_ref[:, 1, 0].astype(F32).reshape(count * own, total).astype(BF)
    prod = mm(left, right, NT)
    out_ref[:, 0] = prod.reshape(count, own, total).astype(BF)


def middle_kernel(p_ref, x_ref, gate_ref, tri_ref, bias_ref, upd_ref, nm_ref, b_ref, acc_ref, bacc_ref):
    blocks, own, cols, width = x_ref.shape
    total = blocks * cols
    hidden = tri_ref.shape[0]
    heads = b_ref.shape[0]
    for t in range(total // 128):
        acc_ref[t] = p_ref[:, t * 128 : (t + 1) * 128].astype(F32)
    for i in range(own):
        prod = jnp.concatenate(
            [acc_ref[t, pl.ds(i, hidden, stride=own), :] for t in range(total // 128)], axis=1
        )
        nprod = layer_norm(prod, axis=0).astype(BF)
        tri = mm(nprod, tri_ref[...], TN)
        x = x_ref[:, i].reshape(total, width).astype(F32)
        normed = layer_norm(x).astype(BF)
        update = sigmoid(mm(normed, gate_ref[...], NN)) * tri
        nm = layer_norm(x + update).astype(BF)
        upd_ref[i] = update
        nm_ref[i] = nm
        bias = mm(bias_ref[...], nm, NT)
        for h in range(heads):
            bacc_ref[h, i : i + 1, :] = bias[h : h + 1]
    b_ref[...] = bacc_ref[...].astype(BF)


def attention_kernel(valid_ref, nm_ref, upd_ref, b_ref, wqk_ref, wvg_ref, wo_ref, out_ref, bt_ref):
    count, heads, own, total = b_ref.shape
    width = wo_ref.shape[0]
    size = width // heads

    @pl.when(pl.program_id(0) == 0)
    def _():
        keep = lax.broadcasted_iota(jnp.int32, (total, 1), 0) < valid_ref[0]
        mask = jnp.where(keep, 0.0, -1000000000.0 * LOG2E).astype(F32)
        for h in range(heads):
            b = b_ref[:, h].astype(F32).reshape(count * own, total)
            bt_ref[h] = jnp.transpose(b) * LOG2E + mask

    nm = nm_ref[0]
    qk = mm(nm, wqk_ref[...], NN)
    query = (qk[:, :width] * (LOG2E * size ** (-0.5))).astype(BF)
    keys = qk[:, width:].astype(BF)
    vg = mm(wvg_ref[...], nm, NT)
    values = vg[:width].astype(BF)
    lane = lax.broadcasted_iota(jnp.int32, (1, width), 1) // size
    outs = []
    for h in range(heads):
        q = jnp.where(lane == h, query, jnp.zeros_like(query))
        s = mm(keys, q, NT) + bt_ref[h]
        p = jnp.exp2(s - jnp.max(s, axis=0, keepdims=True))
        norm = 1.0 / jnp.sum(p, axis=0, keepdims=True)
        o = mm(values[h * size : (h + 1) * size], p.astype(BF), NN)
        outs.append(o * norm)
    gated = (jnp.concatenate(outs, axis=0) * sigmoid(vg[width:])).astype(BF)
    delta = upd_ref[0] + mm(gated, wo_ref[...], TN)
    blocks, _, cols, _ = out_ref.shape
    out_ref[:, 0] = delta.reshape(blocks, cols, width).astype(BF)


VMEM = pl.BlockSpec(memory_space=pltpu.VMEM)
SMEM = pl.BlockSpec(memory_space=pltpu.SMEM)


def cost(flops, nbytes):
    return pl.CostEstimate(flops=flops, bytes_accessed=nbytes, transcendentals=0)


def fast_edges(valid, start, x, weights):
    blocks, own, cols, width = x.shape
    total = blocks * cols
    rows = weights.shape[0] // 2 * own
    return pl.pallas_call(
        edges_kernel,
        out_shape=jax.ShapeDtypeStruct((rows, total), BF),
        in_specs=[SMEM, SMEM, VMEM, VMEM],
        out_specs=VMEM,
        scratch_shapes=[pltpu.VMEM((total // 128, rows, 128), F32)],
        name="edges",
    )(valid, start, x, weights)


def fast_products(edges):
    count, _, chans, own, total = edges.shape
    return pl.pallas_call(
        product_kernel,
        out_shape=jax.ShapeDtypeStruct((count, chans, own, total), BF),
        grid=(chans,),
        in_specs=[pl.BlockSpec((count, 2, 1, own, total), lambda c: (0, 0, c, 0, 0))],
        out_specs=pl.BlockSpec((count, 1, own, total), lambda c: (0, c, 0, 0)),
        name="products",
    )(edges)


def fast_middle(prod, x, tri_gate, tri_out, bias_w, heads):
    blocks, own, cols, width = x.shape
    total = blocks * cols
    rows = prod.shape[0]
    return pl.pallas_call(
        middle_kernel,
        out_shape=(
            jax.ShapeDtypeStruct((own, total, width), F32),
            jax.ShapeDtypeStruct((own, total, width), BF),
            jax.ShapeDtypeStruct((heads, own, total), BF),
        ),
        in_specs=[VMEM] * 5,
        out_specs=(VMEM,) * 3,
        scratch_shapes=[
            pltpu.VMEM((total // 128, rows, 128), F32),
            pltpu.VMEM((heads, own, total), F32),
        ],
        name="middle",
    )(prod, x, tri_gate, tri_out, bias_w)


def fast_attention(valid, nm, upd, bias, wqk, wvg, wo, cols):
    own, total, width = nm.shape
    count, heads = bias.shape[:2]
    blocks = total // cols
    whole = lambda a: pl.BlockSpec(a.shape, lambda i: (0,) * a.ndim)
    row = pl.BlockSpec((1, total, width), lambda i: (i, 0, 0))
    return pl.pallas_call(
        attention_kernel,
        out_shape=jax.ShapeDtypeStruct((blocks, own, cols, width), BF),
        grid=(own,),
        in_specs=[SMEM, row, row, whole(bias), whole(wqk), whole(wvg), whole(wo)],
        out_specs=pl.BlockSpec((blocks, 1, cols, width), lambda i: (0, i, 0, 0)),
        scratch_shapes=[pltpu.VMEM((heads, total, total), F32)],
        name="attention",
    )(valid, nm, upd, bias, wqk, wvg, wo)


def plain_edges(valid, start, x, weights):
    blocks, own, cols, width = x.shape
    total = blocks * cols
    half = weights.shape[0] // 2
    normed = layer_norm(jnp.swapaxes(x, 0, 1).reshape(own, total, width).astype(F32)).astype(BF)
    proj = jnp.einsum("ec,ikc->eik", weights, normed, preferred_element_type=F32)
    keep_k = (jnp.arange(total) < valid[0]).astype(F32)
    keep_i = (start[0] + jnp.arange(own) < valid[0]).astype(F32)
    edge = sigmoid(proj[:half]) * proj[half:] * (keep_i[:, None] * keep_k[None, :])
    return edge.astype(BF).reshape(half * own, total)


def plain_products(edges):
    count, _, chans, own, total = edges.shape
    flat = jnp.transpose(edges, (1, 2, 0, 3, 4)).reshape(2, chans, count * own, total)
    prod = jnp.einsum("cik,cjk->cij", flat[0], flat[1], preferred_element_type=F32).astype(BF)
    return jnp.transpose(prod.reshape(chans, count, own, total), (1, 0, 2, 3))


def plain_middle(prod, x, tri_gate, tri_out, bias_w, heads):
    blocks, own, cols, width = x.shape
    total = blocks * cols
    prod = prod.reshape(tri_out.shape[0], own, total).astype(F32)
    nprod = layer_norm(prod, axis=0).astype(BF)
    tri = jnp.einsum("cij,cd->ijd", nprod, tri_out, preferred_element_type=F32)
    pair = jnp.swapaxes(x, 0, 1).reshape(own, total, width).astype(F32)
    normed = layer_norm(pair).astype(BF)
    update = sigmoid(jnp.dot(normed, tri_gate, preferred_element_type=F32)) * tri
    nm = layer_norm(pair + update).astype(BF)
    bias = jnp.einsum("hc,ijc->hij", bias_w[:heads], nm, preferred_element_type=F32).astype(BF)
    return update, nm, bias


def plain_attention(valid, nm, upd, bias, wqk, wvg, wo, cols):
    own, total, width = nm.shape
    count, heads = bias.shape[:2]
    size = width // heads
    qk = jnp.dot(nm, wqk, preferred_element_type=F32)
    query = (qk[..., :width] * (LOG2E * size ** (-0.5))).astype(BF).reshape(own, total, heads, size)
    keys = qk[..., width:].astype(BF).reshape(own, total, heads, size)
    vg = jnp.einsum("ec,ijc->ije", wvg, nm, preferred_element_type=F32)
    values = vg[..., :width].astype(BF).reshape(own, total, heads, size)
    table = jnp.swapaxes(bias.astype(F32), 0, 1).reshape(heads, total, total) * LOG2E
    mask = jnp.where(jnp.arange(total) < valid[0], 0.0, -1000000000.0 * LOG2E).astype(F32)

    def one(args):
        q, k, v = args
        s = jnp.einsum("jhd,khd->hjk", q, k, preferred_element_type=F32) + table + mask
        p = jnp.exp2(s - jnp.max(s, axis=-1, keepdims=True))
        o = jnp.einsum("hjk,khd->jhd", p.astype(BF), v, preferred_element_type=F32)
        return o / jnp.transpose(jnp.sum(p, axis=-1))[..., None]

    att = lax.map(one, (query, keys, values)).reshape(own, total, width)
    gated = (sigmoid(vg[..., width:]) * att).astype(BF)
    delta = upd + jnp.dot(gated, wo, preferred_element_type=F32)
    return jnp.swapaxes(delta.astype(BF).reshape(own, total // cols, cols, width), 0, 1)


def per_device(pair, valid_length, tri_in, tri_gate, tri_out, att_in, att_bias, att_out):
    rows_dev, cols_dev, width = pair.shape
    hidden = tri_out.shape[0]
    heads = att_bias.shape[1]
    ncol = lax.axis_size("col")
    ndev = ncol * lax.axis_size("row")
    total = cols_dev * ncol
    own = rows_dev // ncol
    chans = hidden // ndev
    both = ("row", "col")
    start = (lax.axis_index(both) * own).astype(jnp.int32).reshape(1)
    fast = own % 8 == 0 and total % 128 == 0
    edges_of = fast_edges if fast else plain_edges
    products_of = fast_products if fast else plain_products
    middle_of = fast_middle if fast else plain_middle
    attention_of = fast_attention if fast else plain_attention

    parts = jnp.transpose(tri_in).reshape(4, ndev, chans, width)
    gates = jnp.stack([parts[0], parts[2]], axis=1)
    vals = jnp.stack([parts[1], parts[3]], axis=1)
    weights = jnp.concatenate([gates.reshape(-1, width), vals.reshape(-1, width)], axis=0)

    x = lax.all_to_all(pair.astype(BF), "col", 0, 0, tiled=True)
    x = x.reshape(ncol, own, cols_dev, width)
    edges = edges_of(valid_length, start, x, weights)
    edges = edges.reshape(ndev, 2 * chans * own, total)
    edges = lax.all_to_all(edges, both, 0, 0, tiled=True)
    prod = products_of(edges.reshape(ndev, 2, chans, own, total))
    prod = prod.reshape(ndev, chans * own, total)
    prod = lax.all_to_all(prod, both, 0, 0, tiled=True).reshape(hidden * own, total)
    pad = -heads % 8
    bias_w = jnp.pad(jnp.transpose(att_bias), ((0, pad), (0, 0)))
    upd, nm, bias = middle_of(prod, x, tri_gate, tri_out, bias_w, heads)
    bias = lax.all_to_all(
        jnp.broadcast_to(bias[None], (ndev, heads, own, total)), both, 0, 0, tiled=True
    )
    wvg = jnp.transpose(att_in[:, 2 * width :])
    delta = attention_of(
        valid_length, nm, upd, bias, att_in[:, : 2 * width], wvg, att_out, cols_dev
    )
    delta = delta.reshape(rows_dev, cols_dev, width)
    delta = lax.all_to_all(delta, "col", 0, 0, tiled=True)
    return pair + delta.astype(F32)


def solution(mesh):
    placed = (P("row", "col", None), P(), P(), P(), P(), P(), P(), P())
    return jax.shard_map(
        per_device, mesh=mesh, in_specs=placed, out_specs=P("row", "col", None), check_vma=False
    )
```

time: 239 us -> 146 us (0.61)
  waiting for transfers between devices: 108 us -> 43.5 us
  matrix products: 47.5 us -> 0 us
  blocking collectives: 9.12 us -> 50 us
  Pallas kernels: 0 us -> 27.9 us
  other arithmetic: 26.6 us -> 4 us
  local copies, waits for them, and re-layouts: 27.6 us -> 6.81 us
  between operations: 14 us -> 0.75 us
  starting transfers between devices: 3.61 us -> 11.8 us
    all_gather x2 -> x0, waiting for transfers between devices: 56.1 us -> none  [the longest x1 36.3 us: per_device(): right_rows = lax.all_gather(right_edges, 'row', axis=0, tiled=True)]
    reduce_scatter x1 -> x0, waiting for transfers between devices: 50 us -> none  [per_device(): lax.psum_scatter(jnp.einsum('jkc,ikc->jic', right_rows, left_edges, prefe...]
    all_to_all x0 -> x2, blocking collectives: none -> 50 us  [the longest x1 31.1 us: per_device(): edges = lax.all_to_all(edges, both, 0, 0, tiled=True)]
    dot_general x24 -> x0, matrix products: 47.5 us -> none  [the longest x8 17.9 us: one_block(): jnp.einsum('ihjk,ikhd->ijhd', expo, values.astype(jnp.float32))]
    all_to_all x1 -> x3, waiting for transfers between devices: 2.24 us -> 43.5 us  [the longest x1 15 us: per_device(): lax.all_to_all(prod, both, 0, 0, tiled=True).reshape(hidden * own, total)]
    pallas_call x0 -> x4, Pallas kernels: none -> 27.9 us  [the longest x1 15.3 us: fast_attention(): pl.pallas_call(attention_kernel, out_shape=jax.ShapeDtypeStruct((blocks,...]
    reduce_sum x13 -> x0, other arithmetic: 10.4 us -> none  [the longest x3 4.18 us: layer_norm(): jnp.mean(center * center, axis=-1, keepdims=True) + 1e-05]
    all_gather x1 -> x0, blocking collectives: 9.12 us -> none  [per_device(): bias_rows = lax.all_gather(bias_local, 'row', axis=0, tiled=True)]
  transfers between devices with their start and end apart: 4 -> 3, of which waited for: 4 -> 3; matrix products, arithmetic and copies ran while one was open for 6% -> 2% of each run, Pallas kernels for 0% -> 0%
where the time goes in v1:
time: 146 us; the launch traced here: 145 us
  blocking collectives  50 us (34%)
  waiting for transfers between devices  43.5 us (30%)
  Pallas kernels  27.9 us (19%)
  starting transfers between devices  11.8 us (8%)
  local copies, waits for them, and re-layouts  6.81 us (5%)
  other arithmetic  4 us (3%)
    all_to_all x1, blocking collectives, per_device(): edges = lax.all_to_all(edges, both, 0, 0, tiled=True)  31.1 us
    all_to_all x1, blocking collectives, per_device(): delta = lax.all_to_all(delta, 'col', 0, 0, tiled=True)  18.9 us
    pallas_call x1, Pallas kernels, fast_attention(): pl.pallas_call(attention_kernel, out_shape=jax.ShapeDtypeStruct((blocks,...  15.3 us
    all_to_all x1, waiting for transfers between devices, per_device(): lax.all_to_all(prod, both, 0, 0, tiled=True).reshape(hidden * own, total)  15 us
    all_to_all x1, waiting for transfers between devices, per_device(): lax.all_to_all(jnp.broadcast_to(bias[None], (ndev, heads, own, total)), b...  14.9 us
    all_to_all x1, waiting for transfers between devices, per_device(): x = lax.all_to_all(pair.astype(BF), 'col', 0, 0, tiled=True)  13.7 us
    all_to_all x1, starting transfers between devices, per_device(): x = lax.all_to_all(pair.astype(BF), 'col', 0, 0, tiled=True)  6.49 us
    pallas_call x1, Pallas kernels, fast_middle(): pl.pallas_call(middle_kernel, out_shape=(jax.ShapeDtypeStruct((own, total...  5.48 us
  transfers between devices with their start and end apart: 3, of which 3 were waited for; matrix products, arithmetic and copies ran while one was open for 2% of the time, Pallas kernels for 0%

profile of v1, /device:TPU:0, one launch (start us, length us, event | category | flops | bytes accessed | tf_op | source)
XLA Modules:
  0.0 144.8 jit_solution(9364283803270054397)
XLA Ops:
  0.0 2.1 %convert_element_type.8 = bf16[64,32,128]{2,1,0:T(8,128)(2,1)} convert(f32[64,32,128]{2,1,0:T(8,128)} %param.8) | non-fusion elementwise | flops 262144 | bytes 1572864 | tf_op jit(solution)/shard_map/convert_element_type | solution.py:270
  2.1 0.0 copy-start.4
  2.1 6.5 %all-to-all-start = ((bf16[64,32,128]{2,1,0:T(8,128)(2,1)}), bf16[64,32,128]{2,1,0:T(8,128)(2,1)S(1)}, u32[]{:S(2)}, u32[]{:S(2)}) async-start(bf16[64,32,128]{2,1,0:T(8,128)(2,1)} %convert_element_type.8), calls=%async_computation | async-start | bytes 1048576 | tf_op jit(solution)/shard_map/all_to_all | solution.py:270
  8.6 0.0 copy-done.4
  8.6 0.1 copy.14
  9.6 0.7 pad_maximum_fusion.w_ref
  10.2 13.7 %all-to-all-done = bf16[64,32,128]{2,1,0:T(8,128)(2,1)S(1)} async-done(((bf16[64,32,128]{2,1,0:T(8,128)(2,1)}), bf16[64,32,128]{2,1,0:T(8,128)(2,1)S(1)}, u32[]{:S(2)}, u32[]{:S(2)}) %all-to-all-start) | async-done | bytes 524320 | tf_op jit(solution)/shard_map/all_to_all | solution.py:270
  23.9 0.0 copy-start
  23.9 0.8 copy-done
  24.8 3.4 %edges.1 = bf16[2048,256]{1,0:T(8,128)(2,1)} custom-call(s32[1]{0:T(128)S(6)} %copy.19.valid_ref, s32[1]{0:T(128)} %bitcast.start_ref, bf16[8,8,32,128]{3,2,1,0:T(8,128)(2,1)} %bitcast.16, bf16[512,128]{1,0:T(8,128)(2,1)} %pad_maximum_fusion.w_ref), custom_call_target="tpu_custom_call" | custom-call | tf_op jit(solution)/shard_map/edges/pallas_call | solution.py:130
  28.2 31.1 %all_to_all.25 = bf16[32,64,256]{2,1,0:T(8,128)(2,1)} all-to-all(bf16[32,64,256]{2,1,0:T(8,128)(2,1)} %bitcast.18), channel_id=1, replica_groups=mesh['row'=4,'col'=8] {'row','col'}, dimensions={0} | all-to-all | bytes 2097152 | tf_op jit(solution)/shard_map/all_to_all | solution.py:274
  59.3 3.7 %products.1 = bf16[32,4,8,256]{3,2,1,0:T(8,128)(2,1)} custom-call(bf16[32,2,4,8,256]{4,3,2,1,0:T(8,128)(2,1)} %bitcast.19), custom_call_target="tpu_custom_call" | custom-call | tf_op jit(solution)/shard_map/products/pallas_call | solution.py:142
  63.0 2.6 %all-to-all-start.2 = ((bf16[32,32,256]{2,1,0:T(8,128)(2,1)}), bf16[32,32,256]{2,1,0:T(8,128)(2,1)S(1)}, u32[]{:S(2)}, u32[]{:S(2)}) async-start(bf16[32,32,256]{2,1,0:T(8,128)(2,1)} %bitcast.20), calls=%async_computation.2 | async-start | bytes 1048576 | tf_op jit(solution)/shard_map/all_to_all | solution.py:277
  65.6 0.0 copy-start.6
  65.6 0.7 copy-done.6
  66.3 0.6 pad.4.bias_ref
  66.9 15.0 %all-to-all-done.2 = bf16[32,32,256]{2,1,0:T(8,128)(2,1)S(1)} async-done(((bf16[32,32,256]{2,1,0:T(8,128)(2,1)}), bf16[32,32,256]{2,1,0:T(8,128)(2,1)S(1)}, u32[]{:S(2)}, u32[]{:S(2)}) %all-to-all-start.2) | async-done | bytes 524320 | tf_op jit(solution)/shard_map/all_to_all | solution.py:277
  81.8 0.0 copy-start.2
  81.8 0.8 copy-done.2
  82.6 5.5 %middle.1 = (f32[8,256,128]{2,1,0:T(8,128)}, bf16[8,256,128]{2,1,0:T(8,128)(2,1)}, bf16[4,8,256]{2,1,0:T(8,128)(2,1)}) custom-call(bf16[1024,256]{1,0:T(8,128)(2,1)} %bitcast.21, bf16[8,8,32,128]{3,2,1,0:T(8,128)(2,1)} %bitcast.17, bf16[128,128]{1,0:T(8,128)(2,1)} %gate_ref.1, bf16[128,128]{1,0:T(8,128)(2,1)} %tri_ref.1, bf16[8,128]{1,0:T(8,128)(2,1)} %pad.4.bias_ref), custom_call_target="tpu_custom_call" | custom-call | tf_op jit(solution)/shard_map/middle/pallas_call | solution.py:156
  88.1 1.6 %broadcast_in_dim.2 = bf16[32,4,8,256]{3,2,1,0:T(8,128)(2,1)} broadcast(bf16[4,8,256]{2,1,0:T(8,128)(2,1)} %get-tuple-element.10), dimensions={1,2,3} | broadcast | bytes 540672 | tf_op jit(solution)/shard_map/broadcast_in_dim | solution.py:282
  89.7 0.0 copy-start.5
  89.7 2.7 %all-to-all-start.3 = ((bf16[32,4,8,256]{3,2,1,0:T(8,128)(2,1)}), bf16[32,4,8,256]{3,2,1,0:T(8,128)(2,1)S(1)}, u32[]{:S(2)}, u32[]{:S(2)}) async-start(bf16[32,4,8,256]{3,2,1,0:T(8,128)(2,1)} %broadcast_in_dim.2), calls=%async_computation.3 | async-start | bytes 1048576 | tf_op jit(solution)/shard_map/all_to_all | solution.py:281
  92.4 0.0 copy-done.5
  92.5 0.6 fusion
  93.1 0.7 copy.18
  93.8 14.9 %all-to-all-done.3.b_ref = bf16[32,4,8,256]{3,2,1,0:T(8,128)(2,1)S(1)} async-done(((bf16[32,4,8,256]{3,2,1,0:T(8,128)(2,1)}), bf16[32,4,8,256]{3,2,1,0:T(8,128)(2,1)S(1)}, u32[]{:S(2)}, u32[]{:S(2)}) %all-to-all-start.3) | async-done | bytes 524320 | tf_op jit(solution)/shard_map/all_to_all | solution.py:281
  108.7 0.0 copy-start.3
  108.7 0.8 copy-done.3
  109.5 15.3 %attention.1 = bf16[8,8,32,128]{3,2,1,0:T(8,128)(2,1)} custom-call(s32[1]{0:T(128)S(6)} %copy.19.valid_ref, bf16[8,256,128]{2,1,0:T(8,128)(2,1)} %get-tuple-element.8.nm_ref, f32[8,256,128]{2,1,0:T(8,128)} %get-tuple-element.9.upd_ref, bf16[32,4,8,256]{3,2,1,0:T(8,128)(2,1)} %copy-done.3, bf16[128,256]{1,0:T(8,128)(2,1)} %get-tuple-element.12.wqk_ref, ...), custom_call_target="tpu_custom_call" | custom-call | tf_op jit(solution)/shard_map/attention/pallas_call | solution.py:179
  124.8 0.0 copy-start.1
  124.8 18.9 %all_to_all.26 = bf16[64,32,128]{2,1,0:T(8,128)(2,1)S(1)} all-to-all(bf16[64,32,128]{2,1,0:T(8,128)(2,1)} %bitcast.22), channel_id=1, replica_groups=mesh['row'=4,'col'=8] {'col'}, dimensions={0} | all-to-all | bytes 1048576 | tf_op jit(solution)/shard_map/all_to_all | solution.py:289
  143.7 0.0 copy-done.1
  143.7 1.1 convert_add_fusion
  (5 shorter events, 0.2 us)
Async XLA Ops:
  2.1 6.5 %copy-start.4 = (bf16[128,512]{1,0:T(8,128)(2,1)S(1)}, bf16[128,512]{1,0:T(8,128)(2,1)}, u32[]{:S(2)}) copy-start(bf16[128,512]{1,0:T(8,128)(2,1)} %param.10) | copy-start | bytes 393220
  2.1 21.8 %all-to-all-start = ((bf16[64,32,128]{2,1,0:T(8,128)(2,1)}), bf16[64,32,128]{2,1,0:T(8,128)(2,1)S(1)}, u32[]{:S(2)}, u32[]{:S(2)}) async-start(bf16[64,32,128]{2,1,0:T(8,128)(2,1)} %convert_element_type.8), calls=%async_computation | async-start | bytes 1048576 | tf_op jit(solution)/shard_map/all_to_all | solution.py:270
  23.9 0.8 copy-start
  63.0 18.8 %all-to-all-start.2 = ((bf16[32,32,256]{2,1,0:T(8,128)(2,1)}), bf16[32,32,256]{2,1,0:T(8,128)(2,1)S(1)}, u32[]{:S(2)}, u32[]{:S(2)}) async-start(bf16[32,32,256]{2,1,0:T(8,128)(2,1)} %bitcast.20), calls=%async_computation.2 | async-start | bytes 1048576 | tf_op jit(solution)/shard_map/all_to_all | solution.py:277
  65.6 0.7 copy-start.6
  81.8 0.8 copy-start.2
  89.7 2.7 %copy-start.5 = (bf16[128,512]{1,0:T(8,128)(2,1)S(1)}, bf16[128,512]{1,0:T(8,128)(2,1)}, u32[]{:S(2)}) copy-start(bf16[128,512]{1,0:T(8,128)(2,1)} %param.13) | copy-start | bytes 393220
  89.7 19.0 %all-to-all-start.3 = ((bf16[32,4,8,256]{3,2,1,0:T(8,128)(2,1)}), bf16[32,4,8,256]{3,2,1,0:T(8,128)(2,1)S(1)}, u32[]{:S(2)}, u32[]{:S(2)}) async-start(bf16[32,4,8,256]{3,2,1,0:T(8,128)(2,1)} %broadcast_in_dim.2), calls=%async_computation.3 | async-start | bytes 1048576 | tf_op jit(solution)/shard_map/all_to_all | solution.py:281
  108.7 0.8 copy-start.3
  124.8 18.9 %copy-start.1 = (f32[64,32,128]{2,1,0:T(8,128)S(1)}, f32[64,32,128]{2,1,0:T(8,128)}, u32[]{:S(2)}) copy-start(f32[64,32,128]{2,1,0:T(8,128)} %param.8) | copy-start | bytes 3145732

commit v2 on v1

v2 whole, which is shorter than its diff:
```python
import functools

import jax
import jax.numpy as jnp
from jax import lax
from jax.experimental import pallas as pl
from jax.experimental.pallas import tpu as pltpu
from jax.sharding import Mesh
from jax.sharding import PartitionSpec as P

BF = jnp.bfloat16
F32 = jnp.float32
LOG2E = 1.4426950408889634
GROUP = 2
NT = (((1,), (1,)), ((), ()))
TN = (((0,), (0,)), ((), ()))
NN = (((1,), (0,)), ((), ()))


def mm(a, b, dims):
    return lax.dot_general(a, b, dims, preferred_element_type=F32)


def sigmoid(v):
    return 0.5 * jnp.tanh(0.5 * v) + 0.5


def layer_norm(v, axis=-1):
    center = v - jnp.mean(v, axis=axis, keepdims=True)
    return center * lax.rsqrt(jnp.mean(center * center, axis=axis, keepdims=True) + 1e-05)


def edge_weights(tri_ref, chans):
    hidden = tri_ref.shape[1] // 4
    new = lax.broadcasted_iota(jnp.int32, (2 * hidden, 2 * hidden), 0)
    old = lax.broadcasted_iota(jnp.int32, (2 * hidden, 2 * hidden), 1)
    side = (new // chans) % 2
    wanted = side * hidden + new // (2 * chans) * chans + new % chans
    pick = jnp.where(old == wanted, 1.0, 0.0).astype(BF)
    tri = [tri_ref[:, n * hidden : (n + 1) * hidden] for n in range(4)]
    gates = mm(pick, jnp.concatenate([tri[0], tri[2]], axis=1), NT)
    vals = mm(pick, jnp.concatenate([tri[1], tri[3]], axis=1), NT)
    return jnp.concatenate([gates, vals], axis=0).astype(BF)


def edges_kernel(valid_ref, x_ref, tri_ref, out_ref, xb_ref, *, chans):
    rows, cols, width = x_ref.shape
    half = out_ref.shape[0]
    step = 16
    span = step * cols
    valid = valid_ref[0]
    row_start = lax.axis_index("row") * rows
    col_start = (lax.axis_index("z") * 2 + lax.axis_index("core")) * cols
    weights = edge_weights(tri_ref, chans)
    token = lax.broadcasted_iota(jnp.int32, (1, span), 1)
    keep_k = (col_start + token % cols < valid).astype(F32)
    for n in range(rows // step):
        x = x_ref[n * step : (n + 1) * step]
        xb_ref[n * step : (n + 1) * step] = x.astype(BF)
        normed = layer_norm(x.reshape(span, width)).astype(BF)
        keep_i = (row_start + n * step + token // cols < valid).astype(F32)
        proj = mm(weights, normed, NT)
        edge = sigmoid(proj[:half]) * proj[half:] * (keep_k * keep_i)
        out_ref[:, n * span : (n + 1) * span] = edge.astype(BF)


def product_kernel(e_ref, out_ref, acc_ref, *, ncol, cols):
    count, both, tokens = e_ref.shape
    chans = both // 2
    quads = ncol // 4
    total = ncol * cols
    rows = tokens // cols
    pitch = acc_ref.shape[1] // both
    lane = lax.broadcasted_iota(jnp.int32, (both, 128), 1)
    low = lane < 64
    even = (lane // 32) % 2 == 0

    def per_row(r, carry):
        for q in range(quads):
            src = [e_ref[r * ncol + q * 4 + g].astype(F32) for g in range(4)]
            for t in range(tokens // 128):
                a = [v[:, t * 128 : (t + 1) * 128] for v in src]
                c = [
                    jnp.where(low, a[0], pltpu.roll(a[2], 64, 1)),
                    jnp.where(low, a[1], pltpu.roll(a[3], 64, 1)),
                    jnp.where(low, pltpu.roll(a[0], 64, 1), a[2]),
                    jnp.where(low, pltpu.roll(a[1], 64, 1), a[3]),
                ]
                d = [
                    jnp.where(even, c[0], pltpu.roll(c[1], 32, 1)),
                    jnp.where(even, pltpu.roll(c[0], 96, 1), c[1]),
                    jnp.where(even, c[2], pltpu.roll(c[3], 32, 1)),
                    jnp.where(even, pltpu.roll(c[2], 96, 1), c[3]),
                ]
                for g in range(4):
                    acc_ref[q, pl.ds(r * rows + t * 4 + g, both, stride=pitch), :] = d[g]
        return carry

    lax.fori_loop(0, count // ncol, per_row, 0)

    def whole(row):
        parts = [acc_ref[q, row * pitch : row * pitch + total, :] for q in range(quads)]
        return jnp.concatenate(parts, axis=1).astype(BF)

    for c in range(chans):
        prod = mm(whole(c), whole(chans + c), NT)
        out_ref[:, c] = prod.reshape(count, total // count, total).astype(BF)


def middle_kernel(p_ref, x_ref, gate_ref, tri_ref, bias_ref, upd_ref, nm_ref, b_ref, acc_ref, bacc_ref):
    blocks, own, cols, width = x_ref.shape
    total = blocks * cols
    hidden = tri_ref.shape[0]
    heads = b_ref.shape[1]
    for t in range(total // 128):
        acc_ref[t] = p_ref[:, t * 128 : (t + 1) * 128].astype(F32)
    for i in range(own):
        prod = jnp.concatenate(
            [acc_ref[t, pl.ds(i, hidden, stride=own), :] for t in range(total // 128)], axis=1
        )
        nprod = layer_norm(prod, axis=0).astype(BF)
        tri = mm(nprod, tri_ref[...], TN)
        x = x_ref[:, i].reshape(total, width).astype(F32)
        normed = layer_norm(x).astype(BF)
        update = sigmoid(mm(normed, gate_ref[...], NN)) * tri
        nm = layer_norm(x + update).astype(BF)
        upd_ref[i] = update
        nm_ref[i] = nm
        bias = mm(bias_ref[...], nm, NT)
        for h in range(heads):
            bacc_ref[h, i : i + 1, :] = bias[h : h + 1]
    bias = bacc_ref[...].astype(BF)
    for n in range(b_ref.shape[0]):
        b_ref[n] = bias


def project_kernel(nm_ref, w_ref, q_ref, k_ref, v_ref, g_ref, *, scale):
    own, total, width = nm_ref.shape
    turned = jnp.transpose(w_ref[:, 2 * width :].astype(F32)).astype(BF)
    for i in range(own):
        nm = nm_ref[i]
        qk = mm(nm, w_ref[:, : 2 * width], NN)
        q_ref[i] = (qk[:, :width] * scale).astype(BF)
        k_ref[i] = qk[:, width:].astype(BF)
        vg = mm(turned, nm, NT)
        v_ref[i] = vg[:width].astype(BF)
        g_ref[i] = sigmoid(vg[width:])


def attention_kernel(
    valid_ref, q_ref, k_ref, v_ref, g_ref, upd_ref, ba_ref, bb_ref, wo_ref, out_ref, bt_ref, tmp_ref, s_ref, p_ref
):
    count, heads, own, total = ba_ref.shape
    width = wo_ref.shape[0]
    size = width // heads
    blocks, _, cols, _ = out_ref.shape
    group = s_ref.shape[0] // heads
    core = lax.axis_index("core")
    keep = lax.broadcasted_iota(jnp.int32, (total, 1), 0) < valid_ref[0]
    mask = jnp.where(keep, 0.0, -1000000000.0 * LOG2E).astype(F32)
    for h in range(heads):
        for n in range(count):
            for ref, side in ((ba_ref, core), (bb_ref, 1 - core)):
                at = pl.multiple_of((2 * n + side) * own, own)
                tmp_ref[h, pl.ds(at, own), :] = ref[n, h].astype(F32)
        bt_ref[h] = jnp.transpose(tmp_ref[h]) * LOG2E + mask
    lane = lax.broadcasted_iota(jnp.int32, (1, width), 1) // size

    def per_group(n, carry):
        tops = []
        norms = []
        for r in range(group):
            query = q_ref[n * group + r]
            for h in range(heads):
                q = jnp.where(lane == h, query, jnp.zeros_like(query))
                s = mm(k_ref[n * group + r], q, NT) + bt_ref[h]
                s_ref[r * heads + h] = s
                tops.append(jnp.max(s, axis=0, keepdims=True))
        for at in range(group * heads):
            p = jnp.exp2(s_ref[at] - tops[at])
            norms.append(1.0 / jnp.sum(p, axis=0, keepdims=True))
            p_ref[at] = p.astype(BF)
        for r in range(group):
            i = n * group + r
            outs = []
            for h in range(heads):
                at = r * heads + h
                outs.append(mm(v_ref[i, h * size : (h + 1) * size], p_ref[at], NN) * norms[at])
            gated = (jnp.concatenate(outs, axis=0) * g_ref[i]).astype(BF)
            delta = upd_ref[i] + mm(gated, wo_ref[...], TN)
            out_ref[:, pl.ds(i, 1)] = delta.reshape(blocks, 1, cols, width).astype(BF)
        return carry

    lax.fori_loop(0, own // group, per_group, 0)


VMEM = pl.BlockSpec(memory_space=pltpu.VMEM)
SMEM = pl.BlockSpec(memory_space=pltpu.SMEM)


def cost(flops, nbytes):
    return pl.CostEstimate(flops=flops, bytes_accessed=nbytes, transcendentals=0)


def fast_edges(valid, pair, tri_in, chans):
    rows, cols, width = pair.shape
    half = tri_in.shape[1] // 2
    return pl.pallas_call(
        functools.partial(edges_kernel, chans=chans),
        out_shape=(
            jax.ShapeDtypeStruct((half, rows * cols), BF),
            jax.ShapeDtypeStruct(pair.shape, BF),
        ),
        in_specs=[SMEM, VMEM, VMEM],
        out_specs=(VMEM, VMEM),
        compiler_params=pltpu.CompilerParams(vmem_limit_bytes=12 << 20),
        name="edges",
    )(valid, pair, tri_in)


def fast_products(edges, ncol, cols):
    count, both, tokens = edges.shape
    total = ncol * cols
    return pl.pallas_call(
        functools.partial(product_kernel, ncol=ncol, cols=cols),
        out_shape=jax.ShapeDtypeStruct((count, both // 2, total // count, total), BF),
        in_specs=[VMEM],
        out_specs=VMEM,
        scratch_shapes=[pltpu.VMEM((ncol // 4, both * (total + 8), 128), F32)],
        compiler_params=pltpu.CompilerParams(vmem_limit_bytes=12 << 20),
        name="products",
    )(edges)


def fast_middle(prod, x, tri_gate, tri_out, bias_w, heads, copies):
    blocks, own, cols, width = x.shape
    total = blocks * cols
    rows = prod.shape[0]
    return pl.pallas_call(
        middle_kernel,
        out_shape=(
            jax.ShapeDtypeStruct((own, total, width), F32),
            jax.ShapeDtypeStruct((own, total, width), BF),
            jax.ShapeDtypeStruct((copies, heads, own, total), BF),
        ),
        in_specs=[VMEM] * 5,
        out_specs=(VMEM,) * 3,
        scratch_shapes=[
            pltpu.VMEM((total // 128, rows, 128), F32),
            pltpu.VMEM((heads, own, total), F32),
        ],
        compiler_params=pltpu.CompilerParams(vmem_limit_bytes=16 << 20),
        name="middle",
    )(prod, x, tri_gate, tri_out, bias_w)


def fast_project(nm, weights, heads):
    own, total, width = nm.shape
    turned = (own, width, total)
    scale = LOG2E * (width // heads) ** (-0.5)
    return pl.pallas_call(
        functools.partial(project_kernel, scale=scale),
        out_shape=(
            jax.ShapeDtypeStruct(nm.shape, BF),
            jax.ShapeDtypeStruct(nm.shape, BF),
            jax.ShapeDtypeStruct(turned, BF),
            jax.ShapeDtypeStruct(turned, F32),
        ),
        in_specs=[VMEM] * 2,
        out_specs=(VMEM,) * 4,
        cost_estimate=cost(8 * own * total * width * width, 16 * own * total * width),
        compiler_params=pltpu.CompilerParams(vmem_limit_bytes=12 << 20),
        name="project",
    )(nm, weights)


def fast_attention(valid, q, k, v, g, upd, mine, other, wo, cols):
    own, total, width = q.shape
    heads = mine.shape[1]
    blocks = total // cols
    return pl.pallas_call(
        attention_kernel,
        out_shape=jax.ShapeDtypeStruct((blocks, own, cols, width), BF),
        in_specs=[SMEM] + [VMEM] * 8,
        out_specs=VMEM,
        scratch_shapes=[pltpu.VMEM((heads, total, total), F32)] * 2
        + [
            pltpu.VMEM((GROUP * heads, total, total), F32),
            pltpu.VMEM((GROUP * heads, total, total), BF),
        ],
        compiler_params=pltpu.CompilerParams(vmem_limit_bytes=20 << 20),
        name="attention",
    )(valid, q, k, v, g, upd, mine, other, wo)


def plain_edges(valid, pair, tri_in, chans):
    rows, cols, width = pair.shape
    half = tri_in.shape[1] // 2
    parts = jnp.transpose(tri_in).reshape(4, -1, chans, width)
    gates = jnp.stack([parts[0], parts[2]], axis=1)
    vals = jnp.stack([parts[1], parts[3]], axis=1)
    weights = jnp.concatenate([gates.reshape(-1, width), vals.reshape(-1, width)], axis=0)
    row_start = lax.axis_index("row") * rows
    col_start = lax.axis_index(("z", "core")) * cols
    normed = layer_norm(pair).astype(BF)
    proj = jnp.einsum("ec,ikc->eik", weights, normed, preferred_element_type=F32)
    keep_k = (col_start + jnp.arange(cols) < valid[0]).astype(F32)
    keep_i = (row_start + jnp.arange(rows) < valid[0]).astype(F32)
    edge = sigmoid(proj[:half]) * proj[half:] * (keep_i[:, None] * keep_k[None, :])
    return edge.astype(BF).reshape(half, rows * cols), pair.astype(BF)


def plain_products(edges, ncol, cols):
    count, both, tokens = edges.shape
    chans, total = both // 2, ncol * cols
    flat = edges.reshape(count // ncol, ncol, 2, chans, tokens // cols, cols)
    flat = jnp.transpose(flat, (2, 3, 0, 4, 1, 5)).reshape(2, chans, total, total)
    prod = jnp.einsum("cik,cjk->cij", flat[0], flat[1], preferred_element_type=F32).astype(BF)
    return jnp.transpose(prod.reshape(chans, count, total // count, total), (1, 0, 2, 3))


def plain_middle(prod, x, tri_gate, tri_out, bias_w, heads, copies):
    blocks, own, cols, width = x.shape
    total = blocks * cols
    prod = prod.reshape(tri_out.shape[0], own, total).astype(F32)
    nprod = layer_norm(prod, axis=0).astype(BF)
    tri = jnp.einsum("cij,cd->ijd", nprod, tri_out, preferred_element_type=F32)
    pair = jnp.swapaxes(x, 0, 1).reshape(own, total, width).astype(F32)
    normed = layer_norm(pair).astype(BF)
    update = sigmoid(jnp.dot(normed, tri_gate, preferred_element_type=F32)) * tri
    nm = layer_norm(pair + update).astype(BF)
    bias = jnp.einsum("hc,ijc->hij", bias_w[:heads], nm, preferred_element_type=F32).astype(BF)
    return update, nm, jnp.broadcast_to(bias[None], (copies,) + bias.shape)


def plain_project(nm, weights, heads):
    own, total, width = nm.shape
    wqk = weights[:, : 2 * width]
    wvg = jnp.transpose(weights[:, 2 * width :])
    scale = LOG2E * (width // heads) ** (-0.5)
    qk = jnp.dot(nm, wqk, preferred_element_type=F32)
    vg = jnp.einsum("ec,ijc->iej", wvg, nm, preferred_element_type=F32)
    query = (qk[..., :width] * scale).astype(BF)
    return query, qk[..., width:].astype(BF), vg[:, :width].astype(BF), sigmoid(vg[:, width:])


def plain_attention(valid, q, k, v, g, upd, mine, other, wo, cols):
    own, total, width = q.shape
    heads = mine.shape[1]
    size = width // heads
    first = jnp.where(lax.axis_index("core") == 0, mine, other)
    second = jnp.where(lax.axis_index("core") == 0, other, mine)
    table = jnp.stack([first, second], axis=1).astype(F32)
    table = jnp.moveaxis(table, 2, 0).reshape(heads, total, total) * LOG2E
    mask = jnp.where(jnp.arange(total) < valid[0], 0.0, -1000000000.0 * LOG2E).astype(F32)

    def one(args):
        q, k, v = args
        s = jnp.einsum("jhd,khd->hjk", q, k, preferred_element_type=F32) + table + mask
        p = jnp.exp2(s - jnp.max(s, axis=-1, keepdims=True))
        o = jnp.einsum("hjk,hdk->hdj", p.astype(BF), v, preferred_element_type=F32)
        return o / jnp.sum(p, axis=-1)[:, None, :]

    split = (own, total, heads, size)
    v = v.reshape(own, heads, size, total)
    att = lax.map(one, (q.reshape(split), k.reshape(split), v)).reshape(own, width, total)
    gated = (g * att).astype(BF)
    delta = upd + jnp.einsum("icj,cd->ijd", gated, wo, preferred_element_type=F32)
    return jnp.swapaxes(delta.astype(BF).reshape(own, total // cols, cols, width), 0, 1)


def per_device(pair, valid_length, tri_in, tri_gate, tri_out, att_in, att_bias, att_out):
    rows_dev, cols_dev, width = pair.shape
    hidden = tri_out.shape[0]
    heads = att_bias.shape[1]
    col = ("z", "core")
    both = ("row", "z", "core")
    chips = ("row", "z")
    ncol = lax.axis_size("z") * lax.axis_size("core")
    ndev = ncol * lax.axis_size("row")
    total = cols_dev * ncol
    own = rows_dev // ncol
    chans = hidden // ndev
    fast = own % 8 == 0 and total % 128 == 0 and chans == 4 and cols_dev == 32 and ncol % 4 == 0
    edges_of = fast_edges if fast else plain_edges
    products_of = fast_products if fast else plain_products
    middle_of = fast_middle if fast else plain_middle
    project_of = fast_project if fast else plain_project
    attention_of = fast_attention if fast else plain_attention

    edges, xb = edges_of(valid_length, pair, tri_in, chans)
    edges = edges.reshape(ndev, 2 * chans, rows_dev * cols_dev)
    edges = lax.all_to_all(edges, both, 0, 0, tiled=True)
    x = lax.all_to_all(xb, col, 0, 0, tiled=True)
    x = x.reshape(ncol, own, cols_dev, width)
    prod = products_of(edges, ncol, cols_dev)
    prod = prod.reshape(ndev, chans * own, total)
    prod = lax.all_to_all(prod, both, 0, 0, tiled=True).reshape(hidden * own, total)
    bias_w = jnp.pad(jnp.transpose(att_bias), ((0, -heads % 8), (0, 0)))
    upd, nm, bias = middle_of(prod, x, tri_gate, tri_out, bias_w, heads, ndev // 2)
    mine = lax.all_to_all(bias, chips, 0, 0, tiled=True)
    other = lax.ppermute(mine, "core", [(0, 1), (1, 0)])
    q, k, v, g = project_of(nm, att_in, heads)
    delta = attention_of(valid_length, q, k, v, g, upd, mine, other, att_out, cols_dev)
    delta = delta.reshape(rows_dev, cols_dev, width)
    delta = lax.all_to_all(delta, col, 0, 0, tiled=True)
    return pair + delta.astype(F32)


def solution(mesh):
    nrow, ncol = mesh.devices.shape
    split = Mesh(mesh.devices.reshape(nrow, ncol // 2, 2), ("row", "z", "core"))
    home = P("row", ("z", "core"), None)
    placed = (home, P(), P(), P(), P(), P(), P(), P())
    return jax.shard_map(
        per_device, mesh=split, in_specs=placed, out_specs=home, check_vma=False
    )
```

time: 146 us -> 120 us (0.82)
  blocking collectives: 50 us -> 66.3 us
  waiting for transfers between devices: 43.5 us -> 27.6 us
  Pallas kernels: 27.9 us -> 14.5 us
  starting transfers between devices: 11.8 us -> 6.23 us
  local copies, waits for them, and re-layouts: 6.81 us -> 2.83 us
  other arithmetic: 4 us -> 1.13 us
    all_to_all x2 -> x1, waiting for transfers between devices: 28.5 us -> 11.3 us  [per_device(): x = lax.all_to_all(xb, col, 0, 0, tiled=True)]
    all_to_all x1 -> x2, blocking collectives: 18.9 us -> 31.7 us  [the longest x1 17.9 us: per_device(): delta = lax.all_to_all(delta, col, 0, 0, tiled=True)]
    pallas_call x1, Pallas kernels: 15.3 us -> 4.88 us  [fast_attention(): pl.pallas_call(attention_kernel, out_shape=jax.ShapeDtypeStruct((blocks,...]
    all_to_all x2 -> x1, starting transfers between devices: 9.22 us -> 3.49 us  [per_device(): x = lax.all_to_all(xb, col, 0, 0, tiled=True)]
    all_to_all x1, blocking collectives: 31.1 us -> 34.6 us  [per_device(): edges = lax.all_to_all(edges, both, 0, 0, tiled=True)]
    convert_element_type x1 -> x0, other arithmetic: 2.11 us -> none  [per_device(): x = lax.all_to_all(pair.astype(BF), 'col', 0, 0, tiled=True)]
    pallas_call x1, Pallas kernels: 5.48 us -> 3.45 us  [fast_middle(): pl.pallas_call(middle_kernel, out_shape=(jax.ShapeDtypeStruct((own, total...]
    broadcast_in_dim x1 -> x0, local copies, waits for them, and re-layouts: 1.57 us -> none  [per_device(): jnp.broadcast_to(bias[None], (ndev, heads, own, total))]
  transfers between devices with their start and end apart: 3 -> 3, of which waited for: 3 -> 3; matrix products, arithmetic and copies ran while one was open for 2% -> 0% of each run, Pallas kernels for 0% -> 4%
where the time goes in v2:
time: 120 us; the launch traced here: 119 us
  blocking collectives  66.3 us (55%)
  waiting for transfers between devices  27.6 us (23%)
  Pallas kernels  14.5 us (12%)
  starting transfers between devices  6.23 us (5%)
  local copies, waits for them, and re-layouts  2.83 us (2%)
    all_to_all x1, blocking collectives, per_device(): edges = lax.all_to_all(edges, both, 0, 0, tiled=True)  34.6 us
    all_to_all x1, blocking collectives, per_device(): delta = lax.all_to_all(delta, col, 0, 0, tiled=True)  17.9 us
    all_to_all x1, waiting for transfers between devices, per_device(): lax.all_to_all(prod, both, 0, 0, tiled=True).reshape(hidden * own, total)  15.5 us
    all_to_all x1, blocking collectives, per_device(): mine = lax.all_to_all(bias, chips, 0, 0, tiled=True)  13.9 us
    all_to_all x1, waiting for transfers between devices, per_device(): x = lax.all_to_all(xb, col, 0, 0, tiled=True)  11.3 us
    pallas_call x1, Pallas kernels, fast_attention(): pl.pallas_call(attention_kernel, out_shape=jax.ShapeDtypeStruct((blocks,...  4.88 us
    pallas_call x1, Pallas kernels, fast_products(): pl.pallas_call(functools.partial(product_kernel, ncol=ncol, cols=cols), o...  3.97 us
    all_to_all x1, starting transfers between devices, per_device(): x = lax.all_to_all(xb, col, 0, 0, tiled=True)  3.49 us
  transfers between devices with their start and end apart: 3, of which 3 were waited for; matrix products, arithmetic and copies ran while one was open for 0% of the time, Pallas kernels for 4%

profile of v2, /device:TPU:0, one launch (start us, length us, event | category | flops | bytes accessed | tf_op | source)
XLA Modules:
  0.0 119.3 jit_solution(17814434505783821710)
XLA Ops:
  0.7 0.0 copy-start
  0.7 1.2 %copy-done = f32[64,32,128]{2,1,0:T(8,128)S(1)} copy-done((f32[64,32,128]{2,1,0:T(8,128)S(1)}, f32[64,32,128]{2,1,0:T(8,128)}, u32[]{:S(2)}) %copy-start) | copy-done | bytes 1048600
  1.9 0.0 copy-start.2
  1.9 0.9 copy-done.2
  2.8 1.4 %edges.1 = (bf16[256,2048]{1,0:T(8,128)(2,1)S(1)}, bf16[64,32,128]{2,1,0:T(8,128)(2,1)}) custom-call(s32[1]{0:T(128)S(6)} %copy.9.valid_ref, f32[64,32,128]{2,1,0:T(8,128)S(1)} %copy-done, bf16[128,512]{1,0:T(8,128)(2,1)S(1)} %copy-done.2), custom_call_target="tpu_custom_call" | custom-call | tf_op jit(solution)/shard_map/edges/pallas_call | solution.py:208
  4.2 34.6 %all_to_all.25.e_ref = bf16[32,8,2048]{2,1,0:T(8,128)(2,1)S(1)} all-to-all(bf16[32,8,2048]{2,1,0:T(8,128)(2,1)S(1)} %bitcast.9), channel_id=1, replica_groups=mesh['row'=4,'z'=4,'core'=2] {'row','z','core'}, dimensions={0} | all-to-all | bytes 2097152 | tf_op jit(solution)/shard_map/all_to_all | solution.py:393
  38.8 3.5 %all-to-all-start.2 = ((bf16[64,32,128]{2,1,0:T(8,128)(2,1)}), bf16[64,32,128]{2,1,0:T(8,128)(2,1)S(1)}, u32[]{:S(2)}, u32[]{:S(2)}) async-start(bf16[64,32,128]{2,1,0:T(8,128)(2,1)} %get-tuple-element.15), calls=%async_computation.2 | async-start | bytes 1048576 | tf_op jit(solution)/shard_map/all_to_all | solution.py:394
  42.3 4.0 %products.1 = bf16[32,4,8,256]{3,2,1,0:T(8,128)(2,1)} custom-call(bf16[32,8,2048]{2,1,0:T(8,128)(2,1)S(1)} %all_to_all.25.e_ref), custom_call_target="tpu_custom_call" | custom-call | tf_op jit(solution)/shard_map/products/pallas_call | solution.py:224
  46.3 11.3 %all-to-all-done.2 = bf16[64,32,128]{2,1,0:T(8,128)(2,1)S(1)} async-done(((bf16[64,32,128]{2,1,0:T(8,128)(2,1)}), bf16[64,32,128]{2,1,0:T(8,128)(2,1)S(1)}, u32[]{:S(2)}, u32[]{:S(2)}) %all-to-all-start.2) | async-done | bytes 524320 | tf_op jit(solution)/shard_map/all_to_all | solution.py:394
  57.6 0.0 copy-start.4
  57.6 0.0 copy-start.5
  57.6 2.7 %all-to-all-start.1 = ((bf16[32,32,256]{2,1,0:T(8,128)(2,1)}), bf16[32,32,256]{2,1,0:T(8,128)(2,1)S(1)}, u32[]{:S(2)}, u32[]{:S(2)}) async-start(bf16[32,32,256]{2,1,0:T(8,128)(2,1)} %bitcast.1), calls=%async_computation.1 | async-start | bytes 1048576 | tf_op jit(solution)/shard_map/all_to_all | solution.py:398
  60.3 0.0 copy-start.7
  60.3 0.7 copy-done.7
  61.0 15.5 %all-to-all-done.1 = bf16[32,32,256]{2,1,0:T(8,128)(2,1)S(1)} async-done(((bf16[32,32,256]{2,1,0:T(8,128)(2,1)}), bf16[32,32,256]{2,1,0:T(8,128)(2,1)S(1)}, u32[]{:S(2)}, u32[]{:S(2)}) %all-to-all-start.1) | async-done | bytes 524320 | tf_op jit(solution)/shard_map/all_to_all | solution.py:398
  76.5 0.0 copy-done.4
  76.6 0.0 copy-done.5
  76.6 3.5 %middle.1 = (f32[8,256,128]{2,1,0:T(8,128)S(1)}, bf16[8,256,128]{2,1,0:T(8,128)(2,1)S(1)}, bf16[16,4,8,256]{3,2,1,0:T(8,128)(2,1)S(1)}) custom-call(bf16[1024,256]{1,0:T(8,128)(2,1)S(1)} %bitcast.8, bf16[8,8,32,128]{3,2,1,0:T(8,128)(2,1)S(1)} %bitcast.7, bf16[128,128]{1,0:T(8,128)(2,1)S(1)} %copy-done.4, bf16[128,128]{1,0:T(8,128)(2,1)S(1)} %copy-done.5, ...), custom_call_target="tpu_custom_call" | custom-call | tf_op jit(solution)/shard_map/middle/pallas_call | solution.py:239
  80.0 0.0 copy-start.6
  80.0 13.9 %all_to_all.26.ba_ref = bf16[16,4,8,256]{3,2,1,0:T(8,128)(2,1)S(1)} all-to-all(bf16[16,4,8,256]{3,2,1,0:T(8,128)(2,1)S(1)} %get-tuple-element.22), channel_id=1, replica_groups=mesh['row'=4,'z'=4,'core'=2] {'row','z'}, dimensions={0} | all-to-all | bytes 524288 | tf_op jit(solution)/shard_map/all_to_all | solution.py:401
  93.9 0.0 collective-permute-start
  93.9 0.0 copy-done.6
  93.9 0.0 copy-start.3
  93.9 0.7 project.1
  94.6 0.8 collective-permute-done.bb_ref
  95.4 0.0 copy-done.3
  95.4 4.9 %attention.1 = bf16[8,8,32,128]{3,2,1,0:T(8,128)(2,1)S(1)} custom-call(s32[1]{0:T(128)S(6)} %copy.9.valid_ref, bf16[8,256,128]{2,1,0:T(8,128)(2,1)S(1)} %get-tuple-element.17.q_ref, bf16[8,256,128]{2,1,0:T(8,128)(2,1)S(1)} %get-tuple-element.18.k_ref, bf16[8,128,256]{2,1,0:T(8,128)(2,1)S(1)} %get-tuple-element.19.v_ref, ...), custom_call_target="tpu_custom_call" | custom-call | tf_op jit(solution)/shard_map/attention/pallas_call | solution.py:281
  100.3 0.0 copy-start.1
  100.3 17.9 %all_to_all.27 = bf16[64,32,128]{2,1,0:T(8,128)(2,1)S(1)} all-to-all(bf16[64,32,128]{2,1,0:T(8,128)(2,1)S(1)} %bitcast.6), channel_id=1, replica_groups=mesh['row'=4,'z'=4,'core'=2] {'z','core'}, dimensions={0} | all-to-all | bytes 1048576 | tf_op jit(solution)/shard_map/all_to_all | solution.py:406
  118.2 0.0 copy-done.1
  118.2 1.1 convert_add_fusion
  (1 shorter events, 0.0 us)
Async XLA Ops:
  0.7 1.2 %copy-start = (f32[64,32,128]{2,1,0:T(8,128)S(1)}, f32[64,32,128]{2,1,0:T(8,128)}, u32[]{:S(2)}) copy-start(f32[64,32,128]{2,1,0:T(8,128)} %x_ref.1) | copy-start | bytes 3145732
  1.9 0.9 copy-start.2
  38.8 18.8 %all-to-all-start.2 = ((bf16[64,32,128]{2,1,0:T(8,128)(2,1)}), bf16[64,32,128]{2,1,0:T(8,128)(2,1)S(1)}, u32[]{:S(2)}, u32[]{:S(2)}) async-start(bf16[64,32,128]{2,1,0:T(8,128)(2,1)} %get-tuple-element.15), calls=%async_computation.2 | async-start | bytes 1048576 | tf_op jit(solution)/shard_map/all_to_all | solution.py:394
  57.6 19.0 %copy-start.4 = (bf16[128,128]{1,0:T(8,128)(2,1)S(1)}, bf16[128,128]{1,0:T(8,128)(2,1)}, u32[]{:S(2)}) copy-start(bf16[128,128]{1,0:T(8,128)(2,1)} %gate_ref.1) | copy-start | bytes 98308
  57.6 19.0 %copy-start.5 = (bf16[128,128]{1,0:T(8,128)(2,1)S(1)}, bf16[128,128]{1,0:T(8,128)(2,1)}, u32[]{:S(2)}) copy-start(bf16[128,128]{1,0:T(8,128)(2,1)} %tri_ref.3) | copy-start | bytes 98308
  57.6 19.0 %all-to-all-start.1 = ((bf16[32,32,256]{2,1,0:T(8,128)(2,1)}), bf16[32,32,256]{2,1,0:T(8,128)(2,1)S(1)}, u32[]{:S(2)}, u32[]{:S(2)}) async-start(bf16[32,32,256]{2,1,0:T(8,128)(2,1)} %bitcast.1), calls=%async_computation.1 | async-start | bytes 1048576 | tf_op jit(solution)/shard_map/all_to_all | solution.py:398
  60.3 0.7 copy-start.7
  80.0 13.9 %copy-start.6 = (bf16[128,512]{1,0:T(8,128)(2,1)S(1)}, bf16[128,512]{1,0:T(8,128)(2,1)}, u32[]{:S(2)}) copy-start(bf16[128,512]{1,0:T(8,128)(2,1)} %w_ref.1) | copy-start | bytes 393220
  93.9 1.5 %collective-permute-start = (bf16[16,4,8,256]{3,2,1,0:T(8,128)(2,1)S(1)}, bf16[16,4,8,256]{3,2,1,0:T(8,128)(2,1)S(1)}, u32[]{:S(2)}, u32[]{:S(2)}) collective-permute-start(bf16[16,4,8,256]{3,2,1,0:T(8,128)(2,1)S(1)} %all_to_all.26.ba_ref), channel_id=1, source_target_pairs={{0,1},{1,0},{2,3},{3,2},{4,5},{5,4},{6,7},{7,6},{8,9},{9,8},{10,11... | collective-permute-start | bytes 786440 | tf_op jit(solution)/shard_map/ppermute | solution.py:402
  93.9 1.5 %copy-start.3 = (bf16[128,128]{1,0:T(8,128)(2,1)S(1)}, bf16[128,128]{1,0:T(8,128)(2,1)}, u32[]{:S(2)}) copy-start(bf16[128,128]{1,0:T(8,128)(2,1)} %wo_ref.1) | copy-start | bytes 98308
  100.3 17.9 %copy-start.1 = (f32[64,32,128]{2,1,0:T(8,128)S(1)}, f32[64,32,128]{2,1,0:T(8,128)}, u32[]{:S(2)}) copy-start(f32[64,32,128]{2,1,0:T(8,128)} %x_ref.1) | copy-start | bytes 3145732

commit v3 on v2

--- a/solution.py
+++ b/solution.py
@@ -7,6 +7,7 @@
 from jax.experimental.pallas import tpu as pltpu
 from jax.sharding import Mesh
 from jax.sharding import PartitionSpec as P
+
 
 BF = jnp.bfloat16
 F32 = jnp.float32
@@ -43,20 +44,23 @@
     return jnp.concatenate([gates, vals], axis=0).astype(BF)
 
 
-def edges_kernel(valid_ref, x_ref, tri_ref, out_ref, xb_ref, *, chans):
+def edges_kernel(valid_ref, x_ref, tri_ref, out_ref, *piece_refs, chans):
     rows, cols, width = x_ref.shape
     half = out_ref.shape[0]
     step = 16
     span = step * cols
     valid = valid_ref[0]
     row_start = lax.axis_index("row") * rows
-    col_start = (lax.axis_index("z") * 2 + lax.axis_index("core")) * cols
+    me = lax.axis_index("z") * 2 + lax.axis_index("core")
+    col_start = me * cols
     weights = edge_weights(tri_ref, chans)
+    own = rows // len(piece_refs)
+    for o, piece in enumerate(piece_refs):
+        piece[...] = x_ref[pl.ds((me ^ o) * own, own)].astype(BF)
     token = lax.broadcasted_iota(jnp.int32, (1, span), 1)
     keep_k = (col_start + token % cols < valid).astype(F32)
     for n in range(rows // step):
         x = x_ref[n * step : (n + 1) * step]
-        xb_ref[n * step : (n + 1) * step] = x.astype(BF)
         normed = layer_norm(x.reshape(span, width)).astype(BF)
         keep_i = (row_start + n * step + token // cols < valid).astype(F32)
         proj = mm(weights, normed, NT)
@@ -107,8 +111,12 @@
         out_ref[:, c] = prod.reshape(count, total // count, total).astype(BF)
 
 
-def middle_kernel(p_ref, x_ref, gate_ref, tri_ref, bias_ref, upd_ref, nm_ref, b_ref, acc_ref, bacc_ref):
+def middle_kernel(p_ref, gate_ref, tri_ref, bias_ref, *refs):
+    pieces, (upd_ref, nm_ref, b_ref, acc_ref, bacc_ref, x_ref) = refs[:-6], refs[-6:]
     blocks, own, cols, width = x_ref.shape
+    me = lax.axis_index("z") * 2 + lax.axis_index("core")
+    for o, piece in enumerate(pieces):
+        x_ref[me ^ o] = piece[...]
     total = blocks * cols
     hidden = tri_ref.shape[0]
     heads = b_ref.shape[1]
@@ -135,7 +143,7 @@
 
 
 def project_kernel(nm_ref, w_ref, q_ref, k_ref, v_ref, g_ref, *, scale):
-    own, total, width = nm_ref.shape
+    own, _, width = nm_ref.shape
     turned = jnp.transpose(w_ref[:, 2 * width :].astype(F32)).astype(BF)
     for i in range(own):
         nm = nm_ref[i]
@@ -202,24 +210,24 @@
     return pl.CostEstimate(flops=flops, bytes_accessed=nbytes, transcendentals=0)
 
 
-def fast_edges(valid, pair, tri_in, chans):
+def fast_edges(valid, pair, tri_in, chans, ncol):
     rows, cols, width = pair.shape
     half = tri_in.shape[1] // 2
     return pl.pallas_call(
         functools.partial(edges_kernel, chans=chans),
         out_shape=(
             jax.ShapeDtypeStruct((half, rows * cols), BF),
-            jax.ShapeDtypeStruct(pair.shape, BF),
+            *[jax.ShapeDtypeStruct((rows // ncol, cols, width), BF)] * ncol,
         ),
         in_specs=[SMEM, VMEM, VMEM],
-        out_specs=(VMEM, VMEM),
+        out_specs=(VMEM,) * (ncol + 1),
         compiler_params=pltpu.CompilerParams(vmem_limit_bytes=12 << 20),
         name="edges",
     )(valid, pair, tri_in)
 
 
 def fast_products(edges, ncol, cols):
-    count, both, tokens = edges.shape
+    count, both, _ = edges.shape
     total = ncol * cols
     return pl.pallas_call(
         functools.partial(product_kernel, ncol=ncol, cols=cols),
@@ -232,8 +240,9 @@
     )(edges)
 
 
-def fast_middle(prod, x, tri_gate, tri_out, bias_w, heads, copies):
-    blocks, own, cols, width = x.shape
+def fast_middle(prod, pieces, tri_gate, tri_out, bias_w, heads, copies):
+    blocks = len(pieces)
+    own, cols, width = pieces[0].shape
     total = blocks * cols
     rows = prod.shape[0]
     return pl.pallas_call(
@@ -243,15 +252,16 @@
             jax.ShapeDtypeStruct((own, total, width), BF),
             jax.ShapeDtypeStruct((copies, heads, own, total), BF),
         ),
-        in_specs=[VMEM] * 5,
+        in_specs=[VMEM] * (4 + blocks),
         out_specs=(VMEM,) * 3,
         scratch_shapes=[
             pltpu.VMEM((total // 128, rows, 128), F32),
             pltpu.VMEM((heads, own, total), F32),
+            pltpu.VMEM((blocks, own, cols, width), BF),
         ],
         compiler_params=pltpu.CompilerParams(vmem_limit_bytes=16 << 20),
         name="middle",
-    )(prod, x, tri_gate, tri_out, bias_w)
+    )(prod, tri_gate, tri_out, bias_w, *pieces)
 
 
 def fast_project(nm, weights, heads):
@@ -293,7 +303,7 @@
     )(valid, q, k, v, g, upd, mine, other, wo)
 
 
-def plain_edges(valid, pair, tri_in, chans):
+def plain_edges(valid, pair, tri_in, chans, ncol):
     rows, cols, width = pair.shape
     half = tri_in.shape[1] // 2
     parts = jnp.transpose(tri_in).reshape(4, -1, chans, width)
@@ -319,7 +329,8 @@
     return jnp.transpose(prod.reshape(chans, count, total // count, total), (1, 0, 2, 3))
 
 
-def plain_middle(prod, x, tri_gate, tri_out, bias_w, heads, copies):
+def plain_middle(prod, pieces, tri_gate, tri_out, bias_w, heads, copies):
+    (x,) = pieces
     blocks, own, cols, width = x.shape
     total = blocks * cols
     prod = prod.reshape(tri_out.shape[0], own, total).astype(F32)
@@ -334,7 +345,7 @@
 
 
 def plain_project(nm, weights, heads):
-    own, total, width = nm.shape
+    _, _, width = nm.shape
     wqk = weights[:, : 2 * width]
     wvg = jnp.transpose(weights[:, 2 * width :])
     scale = LOG2E * (width // heads) ** (-0.5)
@@ -381,23 +392,28 @@
     total = cols_dev * ncol
     own = rows_dev // ncol
     chans = hidden // ndev
-    fast = own % 8 == 0 and total % 128 == 0 and chans == 4 and cols_dev == 32 and ncol % 4 == 0
+    fast = own % 8 == 0 and total % 128 == 0 and chans == 4 and cols_dev == 32 and ncol in (4, 8, 16)
     edges_of = fast_edges if fast else plain_edges
     products_of = fast_products if fast else plain_products
     middle_of = fast_middle if fast else plain_middle
     project_of = fast_project if fast else plain_project
     attention_of = fast_attention if fast else plain_attention
 
-    edges, xb = edges_of(valid_length, pair, tri_in, chans)
+    edges, *pieces = edges_of(valid_length, pair, tri_in, chans, ncol)
     edges = edges.reshape(ndev, 2 * chans, rows_dev * cols_dev)
+    if fast:
+        for o in range(1, ncol):
+            swap = [(n, n ^ o) for n in range(ncol)]
+            pieces[o] = lax.ppermute(pieces[o], col, swap)
+    else:
+        x = lax.all_to_all(pieces[0], col, 0, 0, tiled=True)
+        pieces = [x.reshape(ncol, own, cols_dev, width)]
     edges = lax.all_to_all(edges, both, 0, 0, tiled=True)
-    x = lax.all_to_all(xb, col, 0, 0, tiled=True)
-    x = x.reshape(ncol, own, cols_dev, width)
     prod = products_of(edges, ncol, cols_dev)
     prod = prod.reshape(ndev, chans * own, total)
     prod = lax.all_to_all(prod, both, 0, 0, tiled=True).reshape(hidden * own, total)
     bias_w = jnp.pad(jnp.transpose(att_bias), ((0, -heads % 8), (0, 0)))
-    upd, nm, bias = middle_of(prod, x, tri_gate, tri_out, bias_w, heads, ndev // 2)
+    upd, nm, bias = middle_of(prod, pieces, tri_gate, tri_out, bias_w, heads, ndev // 2)
     mine = lax.all_to_all(bias, chips, 0, 0, tiled=True)
     other = lax.ppermute(mine, "core", [(0, 1), (1, 0)])
     q, k, v, g = project_of(nm, att_in, heads)
@@ -412,6 +428,4 @@
     split = Mesh(mesh.devices.reshape(nrow, ncol // 2, 2), ("row", "z", "core"))
     home = P("row", ("z", "core"), None)
     placed = (home, P(), P(), P(), P(), P(), P(), P())
-    return jax.shard_map(
-        per_device, mesh=split, in_specs=placed, out_specs=home, check_vma=False
-    )
+    return jax.shard_map(per_device, mesh=split, in_specs=placed, out_specs=home, check_vma=False)

time: 120 us -> 115 us (0.958)
  waiting for transfers between devices: 27.6 us -> 13.4 us
  starting transfers between devices: 6.23 us -> 12.9 us
  blocking collectives: 66.3 us -> 70.2 us
    all_to_all x1, waiting for transfers between devices: 15.5 us -> 0.01 us  [per_device(): lax.all_to_all(prod, both, 0, 0, tiled=True).reshape(hidden * own, total)]
    ppermute x0 -> x7, waiting for transfers between devices: none -> 12.6 us  [per_device(): pieces[o] = lax.ppermute(pieces[o], col, swap)]
    all_to_all x1 -> x0, waiting for transfers between devices: 11.3 us -> none  [per_device(): x = lax.all_to_all(xb, col, 0, 0, tiled=True)]
    ppermute x0 -> x7, starting transfers between devices: none -> 10.2 us  [per_device(): pieces[o] = lax.ppermute(pieces[o], col, swap)]
    all_to_all x1, blocking collectives: 13.9 us -> 17.7 us  [per_device(): mine = lax.all_to_all(bias, chips, 0, 0, tiled=True)]
    all_to_all x1 -> x0, starting transfers between devices: 3.49 us -> none  [per_device(): x = lax.all_to_all(xb, col, 0, 0, tiled=True)]
  transfers between devices with their start and end apart: 3 -> 9, of which waited for: 3 -> 4; matrix products, arithmetic and copies ran while one was open for 0% -> 0% of each run, Pallas kernels for 4% -> 1%
where the time goes in v3:
time: 115 us
  blocking collectives  70.2 us (61%)
  Pallas kernels  14.3 us (12%)
  waiting for transfers between devices  13.4 us (12%)
  starting transfers between devices  12.9 us (11%)
  local copies, waits for them, and re-layouts  2.16 us (2%)
    all_to_all x1, blocking collectives, per_device(): edges = lax.all_to_all(edges, both, 0, 0, tiled=True)  34.6 us
    all_to_all x1, blocking collectives, per_device(): delta = lax.all_to_all(delta, col, 0, 0, tiled=True)  17.9 us
    all_to_all x1, blocking collectives, per_device(): mine = lax.all_to_all(bias, chips, 0, 0, tiled=True)  17.7 us
    ppermute x7, waiting for transfers between devices, per_device(): pieces[o] = lax.ppermute(pieces[o], col, swap)  12.6 us
    ppermute x7, starting transfers between devices, per_device(): pieces[o] = lax.ppermute(pieces[o], col, swap)  10.2 us
    pallas_call x1, Pallas kernels, fast_attention(): pl.pallas_call(attention_kernel, out_shape=jax.ShapeDtypeStruct((blocks,...  4.89 us
    pallas_call x1, Pallas kernels, fast_products(): pl.pallas_call(functools.partial(product_kernel, ncol=ncol, cols=cols), o...  3.97 us
    pallas_call x1, Pallas kernels, fast_middle(): pl.pallas_call(middle_kernel, out_shape=(jax.ShapeDtypeStruct((own, total...  3.5 us
  transfers between devices with their start and end apart: 9, of which 4 were waited for; matrix products, arithmetic and copies ran while one was open for 0% of the time, Pallas kernels for 1%

profile of v3, /device:TPU:0, one launch (start us, length us, event | category | flops | bytes accessed | tf_op | source)
XLA Modules:
  0.0 114.8 jit_solution(12166190883388093657)
XLA Ops:
  0.7 0.0 copy-start
  0.7 1.2 %copy-done = f32[64,32,128]{2,1,0:T(8,128)S(1)} copy-done((f32[64,32,128]{2,1,0:T(8,128)S(1)}, f32[64,32,128]{2,1,0:T(8,128)}, u32[]{:S(2)}) %copy-start) | copy-done | bytes 1048600
  1.9 0.0 copy-start.2
  1.9 0.9 copy-done.2
  2.8 1.2 %edges.1 = (bf16[256,2048]{1,0:T(8,128)(2,1)S(1)}, bf16[8,32,128]{2,1,0:T(8,128)(2,1)S(1)}, bf16[8,32,128]{2,1,0:T(8,128)(2,1)S(1)}, bf16[8,32,128]{2,1,0:T(8,12...) custom-call(s32[1]{0:T(128)S(6)} %copy.9.valid_ref, ...), custom_call_target="tpu_custom_call" | custom-call | tf_op jit(solution)/shard_map/edges/pallas_call | solution.py:216
  4.0 34.6 %all_to_all.20.e_ref = bf16[32,8,2048]{2,1,0:T(8,128)(2,1)S(1)} all-to-all(bf16[32,8,2048]{2,1,0:T(8,128)(2,1)S(1)} %bitcast.7), channel_id=1, replica_groups=mesh['row'=4,'z'=4,'core'=2] {'row','z','core'}, dimensions={0} | all-to-all | bytes 2097152 | tf_op jit(solution)/shard_map/all_to_all | solution.py:411
  38.6 4.0 %products.1 = bf16[32,4,8,256]{3,2,1,0:T(8,128)(2,1)} custom-call(bf16[32,8,2048]{2,1,0:T(8,128)(2,1)S(1)} %all_to_all.20.e_ref), custom_call_target="tpu_custom_call" | custom-call | tf_op jit(solution)/shard_map/products/pallas_call | solution.py:232
  42.5 0.0 copy-start.4
  42.5 0.0 copy-start.5
  42.5 2.7 %all-to-all-start.1 = ((bf16[32,32,256]{2,1,0:T(8,128)(2,1)}), bf16[32,32,256]{2,1,0:T(8,128)(2,1)S(1)}, u32[]{:S(2)}, u32[]{:S(2)}) async-start(bf16[32,32,256]{2,1,0:T(8,128)(2,1)} %bitcast.1), calls=%async_computation.1 | async-start | bytes 1048576 | tf_op jit(solution)/shard_map/all_to_all | solution.py:414
  45.3 0.2 collective-permute-start
  45.5 1.7 %collective-permute-start.1 = (bf16[8,32,128]{2,1,0:T(8,128)(2,1)S(1)}, bf16[8,32,128]{2,1,0:T(8,128)(2,1)S(1)}, u32[]{:S(2)}, u32[]{:S(2)}) collective-permute-start(bf16[8,32,128]{2,1,0:T(8,128)(2,1)S(1)} %get-tuple-element.24), channel_id=1, source_target_pairs={{0,2},{1,3},{2,0},{3,1},{4,6},{5,7},{6,4},{7,5},{8,10},{9,11},{10,... | collective-permute-start | bytes 196616 | tf_op jit(solution)/shard_map/ppermute | solution.py:407
  47.2 0.1 collective-permute-start.2
  47.2 2.7 %collective-permute-start.3 = (bf16[8,32,128]{2,1,0:T(8,128)(2,1)S(1)}, bf16[8,32,128]{2,1,0:T(8,128)(2,1)S(1)}, u32[]{:S(2)}, u32[]{:S(2)}) collective-permute-start(bf16[8,32,128]{2,1,0:T(8,128)(2,1)S(1)} %get-tuple-element.26), channel_id=1, source_target_pairs={{0,4},{1,5},{2,6},{3,7},{4,0},{5,1},{6,2},{7,3},{8,12},{9,13},{10,... | collective-permute-start | bytes 196616 | tf_op jit(solution)/shard_map/ppermute | solution.py:407
  49.9 0.0 collective-permute-start.4
  49.9 0.0 collective-permute-done.refs_1_
  49.9 3.6 %collective-permute-start.5 = (bf16[8,32,128]{2,1,0:T(8,128)(2,1)S(1)}, bf16[8,32,128]{2,1,0:T(8,128)(2,1)S(1)}, u32[]{:S(2)}, u32[]{:S(2)}) collective-permute-start(bf16[8,32,128]{2,1,0:T(8,128)(2,1)S(1)} %get-tuple-element.28), channel_id=1, source_target_pairs={{0,6},{1,7},{2,4},{3,5},{4,2},{5,3},{6,0},{7,1},{8,14},{9,15},{10,... | collective-permute-start | bytes 196616 | tf_op jit(solution)/shard_map/ppermute | solution.py:407
  53.5 3.0 %collective-permute-done.1.refs_2_ = bf16[8,32,128]{2,1,0:T(8,128)(2,1)S(1)} collective-permute-done((bf16[8,32,128]{2,1,0:T(8,128)(2,1)S(1)}, bf16[8,32,128]{2,1,0:T(8,128)(2,1)S(1)}, u32[]{:S(2)}, u32[]{:S(2)}) %collective-permute-start.1) | collective-permute-done | bytes 65568 | tf_op jit(solution)/shard_map/ppermute | solution.py:407
  56.5 0.0 copy-start.7
  56.5 2.0 %collective-permute-start.6 = (bf16[8,32,128]{2,1,0:T(8,128)(2,1)S(1)}, bf16[8,32,128]{2,1,0:T(8,128)(2,1)S(1)}, u32[]{:S(2)}, u32[]{:S(2)}) collective-permute-start(bf16[8,32,128]{2,1,0:T(8,128)(2,1)S(1)} %get-tuple-element.29), channel_id=1, source_target_pairs={{0,7},{1,6},{2,5},{3,4},{4,3},{5,2},{6,1},{7,0},{8,15},{9,14},{10,... | collective-permute-start | bytes 196616 | tf_op jit(solution)/shard_map/ppermute | solution.py:407
  58.5 0.0 copy-done.7
  58.5 0.0 collective-permute-done.2.refs_3_
  58.5 9.3 %collective-permute-done.3.refs_4_ = bf16[8,32,128]{2,1,0:T(8,128)(2,1)S(1)} collective-permute-done((bf16[8,32,128]{2,1,0:T(8,128)(2,1)S(1)}, bf16[8,32,128]{2,1,0:T(8,128)(2,1)S(1)}, u32[]{:S(2)}, u32[]{:S(2)}) %collective-permute-start.3) | collective-permute-done | bytes 65568 | tf_op jit(solution)/shard_map/ppermute | solution.py:407
  67.8 0.3 collective-permute-done.4.refs_5_
  68.1 0.0 collective-permute-done.5.refs_6_
  68.1 0.0 collective-permute-done.6.refs_7_
  68.1 0.0 all-to-all-done.1
  68.1 0.0 copy-done.4
  68.1 0.0 copy-done.5
  68.1 3.5 %middle.1 = (f32[8,256,128]{2,1,0:T(8,128)S(1)}, bf16[8,256,128]{2,1,0:T(8,128)(2,1)S(1)}, bf16[16,4,8,256]{3,2,1,0:T(8,128)(2,1)S(1)}) custom-call(bf16[1024,256]{1,0:T(8,128)(2,1)S(1)} %bitcast.6, bf16[128,128]{1,0:T(8,128)(2,1)S(1)} %copy-done.4, bf16[128,128]{1,0:T(8,128)(2,1)S(1)} %copy-done.5, bf16[8,128]{1,0:T(8,128)(2,1)S(1)} %pad.4.bias_ref, ...), custom_call_target="tpu_custom_call" | custom-call | tf_op jit(solution)/shard_map/middle/pallas_call | solution.py:248
  71.6 0.0 copy-start.6
  71.6 17.7 %all_to_all.21.ba_ref = bf16[16,4,8,256]{3,2,1,0:T(8,128)(2,1)S(1)} all-to-all(bf16[16,4,8,256]{3,2,1,0:T(8,128)(2,1)S(1)} %get-tuple-element.36), channel_id=1, replica_groups=mesh['row'=4,'z'=4,'core'=2] {'row','z'}, dimensions={0} | all-to-all | bytes 524288 | tf_op jit(solution)/shard_map/all_to_all | solution.py:417
  89.4 0.0 collective-permute-start.7
  89.4 0.0 copy-done.6
  89.4 0.0 copy-start.3
  89.4 0.7 project.1
  90.2 0.8 collective-permute-done.7.bb_ref
  90.9 0.0 copy-done.3
  90.9 4.9 %attention.1 = bf16[8,8,32,128]{3,2,1,0:T(8,128)(2,1)S(1)} custom-call(s32[1]{0:T(128)S(6)} %copy.9.valid_ref, bf16[8,256,128]{2,1,0:T(8,128)(2,1)S(1)} %get-tuple-element.31.q_ref, bf16[8,256,128]{2,1,0:T(8,128)(2,1)S(1)} %get-tuple-element.32.k_ref, bf16[8,128,256]{2,1,0:T(8,128)(2,1)S(1)} %get-tuple-element.33.v_ref, ...), custom_call_target="tpu_custom_call" | custom-call | tf_op jit(solution)/shard_map/attention/pallas_call | solution.py:291
  95.8 0.0 copy-start.1
  95.8 17.9 %all_to_all.22 = bf16[64,32,128]{2,1,0:T(8,128)(2,1)S(1)} all-to-all(bf16[64,32,128]{2,1,0:T(8,128)(2,1)S(1)} %bitcast.5), channel_id=1, replica_groups=mesh['row'=4,'z'=4,'core'=2] {'z','core'}, dimensions={0} | all-to-all | bytes 1048576 | tf_op jit(solution)/shard_map/all_to_all | solution.py:422
  113.7 0.0 copy-done.1
  113.7 1.1 convert_add_fusion
  (1 shorter events, 0.0 us)
Async XLA Ops:
  0.7 1.2 %copy-start = (f32[64,32,128]{2,1,0:T(8,128)S(1)}, f32[64,32,128]{2,1,0:T(8,128)}, u32[]{:S(2)}) copy-start(f32[64,32,128]{2,1,0:T(8,128)} %x_ref.1) | copy-start | bytes 3145732
  1.9 0.9 copy-start.2
  42.5 25.6 %copy-start.4 = (bf16[128,128]{1,0:T(8,128)(2,1)S(1)}, bf16[128,128]{1,0:T(8,128)(2,1)}, u32[]{:S(2)}) copy-start(bf16[128,128]{1,0:T(8,128)(2,1)} %gate_ref.1) | copy-start | bytes 98308
  42.5 25.6 %copy-start.5 = (bf16[128,128]{1,0:T(8,128)(2,1)S(1)}, bf16[128,128]{1,0:T(8,128)(2,1)}, u32[]{:S(2)}) copy-start(bf16[128,128]{1,0:T(8,128)(2,1)} %tri_ref.3) | copy-start | bytes 98308
  42.5 25.6 %all-to-all-start.1 = ((bf16[32,32,256]{2,1,0:T(8,128)(2,1)}), bf16[32,32,256]{2,1,0:T(8,128)(2,1)S(1)}, u32[]{:S(2)}, u32[]{:S(2)}) async-start(bf16[32,32,256]{2,1,0:T(8,128)(2,1)} %bitcast.1), calls=%async_computation.1 | async-start | bytes 1048576 | tf_op jit(solution)/shard_map/all_to_all | solution.py:414
  45.3 4.6 %collective-permute-start = (bf16[8,32,128]{2,1,0:T(8,128)(2,1)S(1)}, bf16[8,32,128]{2,1,0:T(8,128)(2,1)S(1)}, u32[]{:S(2)}, u32[]{:S(2)}) collective-permute-start(bf16[8,32,128]{2,1,0:T(8,128)(2,1)S(1)} %get-tuple-element.23), channel_id=1, source_target_pairs={{0,1},{1,0},{2,3},{3,2},{4,5},{5,4},{6,7},{7,6},{8,9},{9,8},{10,11... | collective-permute-start | bytes 196616 | tf_op jit(solution)/shard_map/ppermute | solution.py:407
  45.5 11.0 %collective-permute-start.1 = (bf16[8,32,128]{2,1,0:T(8,128)(2,1)S(1)}, bf16[8,32,128]{2,1,0:T(8,128)(2,1)S(1)}, u32[]{:S(2)}, u32[]{:S(2)}) collective-permute-start(bf16[8,32,128]{2,1,0:T(8,128)(2,1)S(1)} %get-tuple-element.24), channel_id=1, source_target_pairs={{0,2},{1,3},{2,0},{3,1},{4,6},{5,7},{6,4},{7,5},{8,10},{9,11},{10,... | collective-permute-start | bytes 196616 | tf_op jit(solution)/shard_map/ppermute | solution.py:407
  47.2 11.3 %collective-permute-start.2 = (bf16[8,32,128]{2,1,0:T(8,128)(2,1)S(1)}, bf16[8,32,128]{2,1,0:T(8,128)(2,1)S(1)}, u32[]{:S(2)}, u32[]{:S(2)}) collective-permute-start(bf16[8,32,128]{2,1,0:T(8,128)(2,1)S(1)} %get-tuple-element.25), channel_id=1, source_target_pairs={{0,3},{1,2},{2,1},{3,0},{4,7},{5,6},{6,5},{7,4},{8,11},{9,10},{10,... | collective-permute-start | bytes 196616 | tf_op jit(solution)/shard_map/ppermute | solution.py:407
  47.2 20.6 %collective-permute-start.3 = (bf16[8,32,128]{2,1,0:T(8,128)(2,1)S(1)}, bf16[8,32,128]{2,1,0:T(8,128)(2,1)S(1)}, u32[]{:S(2)}, u32[]{:S(2)}) collective-permute-start(bf16[8,32,128]{2,1,0:T(8,128)(2,1)S(1)} %get-tuple-element.26), channel_id=1, source_target_pairs={{0,4},{1,5},{2,6},{3,7},{4,0},{5,1},{6,2},{7,3},{8,12},{9,13},{10,... | collective-permute-start | bytes 196616 | tf_op jit(solution)/shard_map/ppermute | solution.py:407
  49.9 18.2 %collective-permute-start.4 = (bf16[8,32,128]{2,1,0:T(8,128)(2,1)S(1)}, bf16[8,32,128]{2,1,0:T(8,128)(2,1)S(1)}, u32[]{:S(2)}, u32[]{:S(2)}) collective-permute-start(bf16[8,32,128]{2,1,0:T(8,128)(2,1)S(1)} %get-tuple-element.27), channel_id=1, source_target_pairs={{0,5},{1,4},{2,7},{3,6},{4,1},{5,0},{6,3},{7,2},{8,13},{9,12},{10,... | collective-permute-start | bytes 196616 | tf_op jit(solution)/shard_map/ppermute | solution.py:407
  49.9 18.2 %collective-permute-start.5 = (bf16[8,32,128]{2,1,0:T(8,128)(2,1)S(1)}, bf16[8,32,128]{2,1,0:T(8,128)(2,1)S(1)}, u32[]{:S(2)}, u32[]{:S(2)}) collective-permute-start(bf16[8,32,128]{2,1,0:T(8,128)(2,1)S(1)} %get-tuple-element.28), channel_id=1, source_target_pairs={{0,6},{1,7},{2,4},{3,5},{4,2},{5,3},{6,0},{7,1},{8,14},{9,15},{10,... | collective-permute-start | bytes 196616 | tf_op jit(solution)/shard_map/ppermute | solution.py:407
  56.5 2.0 %copy-start.7 = (bf16[128,4]{0,1:T(4,128)(2,1)S(1)}, bf16[128,4]{0,1:T(4,128)(2,1)}, u32[]{:S(2)}) copy-start(bf16[128,4]{0,1:T(4,128)(2,1)} %param.14) | copy-start | bytes 3076
  56.5 11.6 %collective-permute-start.6 = (bf16[8,32,128]{2,1,0:T(8,128)(2,1)S(1)}, bf16[8,32,128]{2,1,0:T(8,128)(2,1)S(1)}, u32[]{:S(2)}, u32[]{:S(2)}) collective-permute-start(bf16[8,32,128]{2,1,0:T(8,128)(2,1)S(1)} %get-tuple-element.29), channel_id=1, source_target_pairs={{0,7},{1,6},{2,5},{3,4},{4,3},{5,2},{6,1},{7,0},{8,15},{9,14},{10,... | collective-permute-start | bytes 196616 | tf_op jit(solution)/shard_map/ppermute | solution.py:407
  71.6 17.8 %copy-start.6 = (bf16[128,512]{1,0:T(8,128)(2,1)S(1)}, bf16[128,512]{1,0:T(8,128)(2,1)}, u32[]{:S(2)}) copy-start(bf16[128,512]{1,0:T(8,128)(2,1)} %w_ref.1) | copy-start | bytes 393220
  89.4 1.5 %collective-permute-start.7 = (bf16[16,4,8,256]{3,2,1,0:T(8,128)(2,1)S(1)}, bf16[16,4,8,256]{3,2,1,0:T(8,128)(2,1)S(1)}, u32[]{:S(2)}, u32[]{:S(2)}) collective-permute-start(bf16[16,4,8,256]{3,2,1,0:T(8,128)(2,1)S(1)} %all_to_all.21.ba_ref), channel_id=1, source_target_pairs={{0,1},{1,0},{2,3},{3,2},{4,5},{5,4},{6,7},{7,6},{8,9},{9,8},{10,11... | collective-permute-start | bytes 786440 | tf_op jit(solution)/shard_map/ppermute | solution.py:418
  89.4 1.5 %copy-start.3 = (bf16[128,128]{1,0:T(8,128)(2,1)S(1)}, bf16[128,128]{1,0:T(8,128)(2,1)}, u32[]{:S(2)}) copy-start(bf16[128,128]{1,0:T(8,128)(2,1)} %wo_ref.1) | copy-start | bytes 98308
  95.8 17.9 %copy-start.1 = (f32[64,32,128]{2,1,0:T(8,128)S(1)}, f32[64,32,128]{2,1,0:T(8,128)}, u32[]{:S(2)}) copy-start(f32[64,32,128]{2,1,0:T(8,128)} %x_ref.1) | copy-start | bytes 3145732

commit v4 on v3

--- a/solution.py
+++ b/solution.py
@@ -74,30 +74,25 @@
     quads = ncol // 4
     total = ncol * cols
     rows = tokens // cols
+    tiles = tokens // 128
     pitch = acc_ref.shape[1] // both
-    lane = lax.broadcasted_iota(jnp.int32, (both, 128), 1)
-    low = lane < 64
-    even = (lane // 32) % 2 == 0
+    old = lax.broadcasted_iota(jnp.int32, (512, 512), 0)
+    new = lax.broadcasted_iota(jnp.int32, (512, 512), 1)
+    wanted = new // 32 % 4 * 128 + new // 128 * 32 + new % 32
+    turn = jnp.where(old == wanted, 1.0, 0.0).astype(BF)
 
     def per_row(r, carry):
         for q in range(quads):
-            src = [e_ref[r * ncol + q * 4 + g].astype(F32) for g in range(4)]
-            for t in range(tokens // 128):
-                a = [v[:, t * 128 : (t + 1) * 128] for v in src]
-                c = [
-                    jnp.where(low, a[0], pltpu.roll(a[2], 64, 1)),
-                    jnp.where(low, a[1], pltpu.roll(a[3], 64, 1)),
-                    jnp.where(low, pltpu.roll(a[0], 64, 1), a[2]),
-                    jnp.where(low, pltpu.roll(a[1], 64, 1), a[3]),
-                ]
-                d = [
-                    jnp.where(even, c[0], pltpu.roll(c[1], 32, 1)),
-                    jnp.where(even, pltpu.roll(c[0], 96, 1), c[1]),
-                    jnp.where(even, c[2], pltpu.roll(c[3], 32, 1)),
-                    jnp.where(even, pltpu.roll(c[2], 96, 1), c[3]),
-                ]
+            sides = []
+            for g in range(4):
+                v = e_ref[r * ncol + q * 4 + g].astype(F32)
+                v = [v[:, t * 128 : (t + 1) * 128] for t in range(tiles)]
+                sides.append(jnp.concatenate(v, axis=0).astype(BF))
+            turned = mm(jnp.concatenate(sides, axis=1), turn, NN)
+            for t in range(tiles):
                 for g in range(4):
-                    acc_ref[q, pl.ds(r * rows + t * 4 + g, both, stride=pitch), :] = d[g]
+                    part = turned[t * both : (t + 1) * both, g * 128 : (g + 1) * 128]
+                    acc_ref[q, pl.ds(r * rows + t * 4 + g, both, stride=pitch), :] = part
         return carry
 
     lax.fori_loop(0, count // ncol, per_row, 0)
@@ -155,14 +150,8 @@
         g_ref[i] = sigmoid(vg[width:])
 
 
-def attention_kernel(
-    valid_ref, q_ref, k_ref, v_ref, g_ref, upd_ref, ba_ref, bb_ref, wo_ref, out_ref, bt_ref, tmp_ref, s_ref, p_ref
-):
+def bias_table(valid_ref, ba_ref, bb_ref, bt_ref, tmp_ref):
     count, heads, own, total = ba_ref.shape
-    width = wo_ref.shape[0]
-    size = width // heads
-    blocks, _, cols, _ = out_ref.shape
-    group = s_ref.shape[0] // heads
     core = lax.axis_index("core")
     keep = lax.broadcasted_iota(jnp.int32, (total, 1), 0) < valid_ref[0]
     mask = jnp.where(keep, 0.0, -1000000000.0 * LOG2E).astype(F32)
@@ -172,16 +161,25 @@
                 at = pl.multiple_of((2 * n + side) * own, own)
                 tmp_ref[h, pl.ds(at, own), :] = ref[n, h].astype(F32)
         bt_ref[h] = jnp.transpose(tmp_ref[h]) * LOG2E + mask
+
+
+def attend_rows(q_ref, k_ref, v_ref, g_ref, upd_ref, wo_ref, out_ref, bt_ref, s_ref, p_ref):
+    width = wo_ref.shape[0]
+    heads = bt_ref.shape[0]
+    size = width // heads
+    blocks, count, cols, _ = out_ref.shape
+    group = s_ref.shape[0] // heads
     lane = lax.broadcasted_iota(jnp.int32, (1, width), 1) // size
 
     def per_group(n, carry):
         tops = []
         norms = []
         for r in range(group):
-            query = q_ref[n * group + r]
+            i = n * group + r
+            query = q_ref[i]
             for h in range(heads):
                 q = jnp.where(lane == h, query, jnp.zeros_like(query))
-                s = mm(k_ref[n * group + r], q, NT) + bt_ref[h]
+                s = mm(k_ref[i], q, NT) + bt_ref[h]
                 s_ref[r * heads + h] = s
                 tops.append(jnp.max(s, axis=0, keepdims=True))
         for at in range(group * heads):
@@ -199,7 +197,27 @@
             out_ref[:, pl.ds(i, 1)] = delta.reshape(blocks, 1, cols, width).astype(BF)
         return carry
 
-    lax.fori_loop(0, own // group, per_group, 0)
+    lax.fori_loop(0, count // group, per_group, 0)
+
+
+def attention_kernel(
+    valid_ref, q_ref, k_ref, v_ref, g_ref, upd_ref, ba_ref, bb_ref, wo_ref, *refs
+):
+    pieces, (out_ref, bt_ref, tmp_ref, s_ref, p_ref) = refs[:-5], refs[-5:]
+    bias_table(valid_ref, ba_ref, bb_ref, bt_ref, tmp_ref)
+    attend_rows(q_ref, k_ref, v_ref, g_ref, upd_ref, wo_ref, out_ref, bt_ref, s_ref, p_ref)
+    me = lax.axis_index("z") * 2 + lax.axis_index("core")
+    for o, piece in enumerate(pieces):
+        piece[...] = out_ref[me ^ o]
+
+
+def add_kernel(x_ref, *refs):
+    pieces, out_ref = refs[:-1], refs[-1]
+    own = pieces[0].shape[0]
+    me = lax.axis_index("z") * 2 + lax.axis_index("core")
+    for o, piece in enumerate(pieces):
+        rows = pl.ds((me ^ o) * own, own)
+        out_ref[rows] = x_ref[rows] + piece[...].astype(F32)
 
 
 VMEM = pl.BlockSpec(memory_space=pltpu.VMEM)
@@ -284,23 +302,40 @@
     )(nm, weights)
 
 
-def fast_attention(valid, q, k, v, g, upd, mine, other, wo, cols):
+def fast_attention(valid, q, k, v, g, upd, mine, other, wo, cols, col):
     own, total, width = q.shape
     heads = mine.shape[1]
     blocks = total // cols
-    return pl.pallas_call(
+    pieces = pl.pallas_call(
         attention_kernel,
-        out_shape=jax.ShapeDtypeStruct((blocks, own, cols, width), BF),
+        out_shape=(jax.ShapeDtypeStruct((own, cols, width), BF),) * blocks,
         in_specs=[SMEM] + [VMEM] * 8,
-        out_specs=VMEM,
-        scratch_shapes=[pltpu.VMEM((heads, total, total), F32)] * 2
-        + [
+        out_specs=(VMEM,) * blocks,
+        scratch_shapes=[
+            pltpu.VMEM((blocks, own, cols, width), BF),
+            pltpu.VMEM((heads, total, total), F32),
+            pltpu.VMEM((heads, total, total), F32),
             pltpu.VMEM((GROUP * heads, total, total), F32),
             pltpu.VMEM((GROUP * heads, total, total), BF),
         ],
         compiler_params=pltpu.CompilerParams(vmem_limit_bytes=20 << 20),
         name="attention",
     )(valid, q, k, v, g, upd, mine, other, wo)
+    pieces = list(pieces)
+    for o in range(1, blocks):
+        pieces[o] = lax.ppermute(pieces[o], col, [(n, n ^ o) for n in range(blocks)])
+    return pieces
+
+
+def fast_add(pair, pieces):
+    return pl.pallas_call(
+        add_kernel,
+        out_shape=jax.ShapeDtypeStruct(pair.shape, F32),
+        in_specs=[VMEM] * (1 + len(pieces)),
+        out_specs=VMEM,
+        compiler_params=pltpu.CompilerParams(vmem_limit_bytes=12 << 20),
+        name="add",
+    )(pair, *pieces)
 
 
 def plain_edges(valid, pair, tri_in, chans, ncol):
@@ -397,7 +432,6 @@
     products_of = fast_products if fast else plain_products
     middle_of = fast_middle if fast else plain_middle
     project_of = fast_project if fast else plain_project
-    attention_of = fast_attention if fast else plain_attention
 
     edges, *pieces = edges_of(valid_length, pair, tri_in, chans, ncol)
     edges = edges.reshape(ndev, 2 * chans, rows_dev * cols_dev)
@@ -417,7 +451,12 @@
     mine = lax.all_to_all(bias, chips, 0, 0, tiled=True)
     other = lax.ppermute(mine, "core", [(0, 1), (1, 0)])
     q, k, v, g = project_of(nm, att_in, heads)
-    delta = attention_of(valid_length, q, k, v, g, upd, mine, other, att_out, cols_dev)
+    if fast:
+        pieces = fast_attention(
+            valid_length, q, k, v, g, upd, mine, other, att_out, cols_dev, col
+        )
+        return fast_add(pair, pieces)
+    delta = plain_attention(valid_length, q, k, v, g, upd, mine, other, att_out, cols_dev)
     delta = delta.reshape(rows_dev, cols_dev, width)
     delta = lax.all_to_all(delta, col, 0, 0, tiled=True)
     return pair + delta.astype(F32)

time: 115 us -> 110 us (0.957)
  blocking collectives: 70.2 us -> 52.3 us
  starting transfers between devices: 12.9 us -> 20.5 us
  waiting for transfers between devices: 13.4 us -> 19.5 us
    all_to_all x1 -> x0, blocking collectives: 17.9 us -> none  [per_device(): delta = lax.all_to_all(delta, col, 0, 0, tiled=True)]
    ppermute x0 -> x7, starting transfers between devices: none -> 7.55 us  [fast_attention(): lax.ppermute(pieces[o], col, [(n, n ^ o) for n in range(blocks)])]
    ppermute x0 -> x7, waiting for transfers between devices: none -> 6.14 us  [fast_attention(): lax.ppermute(pieces[o], col, [(n, n ^ o) for n in range(blocks)])]
    pallas_call x1, Pallas kernels: 3.97 us -> 2.61 us  [fast_products(): pl.pallas_call(functools.partial(product_kernel, ncol=ncol, cols=cols), o...]
    pallas_call x1 -> x2, Pallas kernels: 4.89 us -> 6 us  [the longest x1 4.94 us: fast_attention(): pl.pallas_call(attention_kernel, out_shape=(jax.ShapeDtypeStruct((own, co...]
  transfers between devices with their start and end apart: 9 -> 16, of which waited for: 4 -> 7; matrix products, arithmetic and copies ran while one was open for 0% -> 0% of each run, Pallas kernels for 1% -> 1%
where the time goes in v4:
time: 110 us; the launch traced here: 109 us
  blocking collectives  52.3 us (48%)
  starting transfers between devices  20.5 us (19%)
  waiting for transfers between devices  19.5 us (18%)
  Pallas kernels  14 us (13%)
  local copies, waits for them, and re-layouts  2.15 us (2%)
    all_to_all x1, blocking collectives, per_device(): edges = lax.all_to_all(edges, both, 0, 0, tiled=True)  34.6 us
    all_to_all x1, blocking collectives, per_device(): mine = lax.all_to_all(bias, chips, 0, 0, tiled=True)  17.7 us
    ppermute x7, waiting for transfers between devices, per_device(): pieces[o] = lax.ppermute(pieces[o], col, swap)  12.6 us
    ppermute x7, starting transfers between devices, per_device(): pieces[o] = lax.ppermute(pieces[o], col, swap)  10.2 us
    ppermute x7, starting transfers between devices, fast_attention(): lax.ppermute(pieces[o], col, [(n, n ^ o) for n in range(blocks)])  7.55 us
    ppermute x7, waiting for transfers between devices, fast_attention(): lax.ppermute(pieces[o], col, [(n, n ^ o) for n in range(blocks)])  6.14 us
    pallas_call x1, Pallas kernels, fast_attention(): pl.pallas_call(attention_kernel, out_shape=(jax.ShapeDtypeStruct((own, co...  4.94 us
    pallas_call x1, Pallas kernels, fast_middle(): pl.pallas_call(middle_kernel, out_shape=(jax.ShapeDtypeStruct((own, total...  3.5 us
  transfers between devices with their start and end apart: 16, of which 7 were waited for; matrix products, arithmetic and copies ran while one was open for 0% of the time, Pallas kernels for 1%

profile of v4, /device:TPU:0, one launch (start us, length us, event | category | flops | bytes accessed | tf_op | source)
XLA Modules:
  0.0 109.3 jit_solution(17367284148160184367)
XLA Ops:
  0.7 0.0 copy-start
  0.7 1.2 %copy-done = f32[64,32,128]{2,1,0:T(8,128)S(1)} copy-done((f32[64,32,128]{2,1,0:T(8,128)S(1)}, f32[64,32,128]{2,1,0:T(8,128)}, u32[]{:S(2)}) %copy-start) | copy-done | bytes 1048600
  1.9 0.0 copy-start.2
  1.9 0.9 copy-done.2
  2.8 1.2 %edges.1 = (bf16[256,2048]{1,0:T(8,128)(2,1)S(1)}, bf16[8,32,128]{2,1,0:T(8,128)(2,1)S(1)}, bf16[8,32,128]{2,1,0:T(8,128)(2,1)S(1)}, bf16[8,32,128]{2,1,0:T(8,12...) custom-call(s32[1]{0:T(128)S(6)} %copy.9.valid_ref, ...), custom_call_target="tpu_custom_call" | custom-call | tf_op jit(solution)/shard_map/edges/pallas_call | solution.py:234
  4.0 34.6 %all_to_all.15.e_ref = bf16[32,8,2048]{2,1,0:T(8,128)(2,1)S(1)} all-to-all(bf16[32,8,2048]{2,1,0:T(8,128)(2,1)S(1)} %bitcast.5), channel_id=1, replica_groups=mesh['row'=4,'z'=4,'core'=2] {'row','z','core'}, dimensions={0} | all-to-all | bytes 2097152 | tf_op jit(solution)/shard_map/all_to_all | solution.py:445
  38.6 2.6 %products.1 = bf16[32,4,8,256]{3,2,1,0:T(8,128)(2,1)} custom-call(bf16[32,8,2048]{2,1,0:T(8,128)(2,1)S(1)} %all_to_all.15.e_ref), custom_call_target="tpu_custom_call" | custom-call | tf_op jit(solution)/shard_map/products/pallas_call | solution.py:250
  41.2 0.0 copy-start.4
  41.2 0.0 copy-start.5
  41.2 2.7 %all-to-all-start.1 = ((bf16[32,32,256]{2,1,0:T(8,128)(2,1)}), bf16[32,32,256]{2,1,0:T(8,128)(2,1)S(1)}, u32[]{:S(2)}, u32[]{:S(2)}) async-start(bf16[32,32,256]{2,1,0:T(8,128)(2,1)} %bitcast.1), calls=%async_computation.1 | async-start | bytes 1048576 | tf_op jit(solution)/shard_map/all_to_all | solution.py:448
  43.9 0.2 collective-permute-start
  44.1 1.7 %collective-permute-start.1 = (bf16[8,32,128]{2,1,0:T(8,128)(2,1)S(1)}, bf16[8,32,128]{2,1,0:T(8,128)(2,1)S(1)}, u32[]{:S(2)}, u32[]{:S(2)}) collective-permute-start(bf16[8,32,128]{2,1,0:T(8,128)(2,1)S(1)} %get-tuple-element.32), channel_id=1, source_target_pairs={{0,2},{1,3},{2,0},{3,1},{4,6},{5,7},{6,4},{7,5},{8,10},{9,11},{10,... | collective-permute-start | bytes 196616 | tf_op jit(solution)/shard_map/ppermute | solution.py:441
  45.8 0.1 collective-permute-start.2
  45.8 2.7 %collective-permute-start.3 = (bf16[8,32,128]{2,1,0:T(8,128)(2,1)S(1)}, bf16[8,32,128]{2,1,0:T(8,128)(2,1)S(1)}, u32[]{:S(2)}, u32[]{:S(2)}) collective-permute-start(bf16[8,32,128]{2,1,0:T(8,128)(2,1)S(1)} %get-tuple-element.34), channel_id=1, source_target_pairs={{0,4},{1,5},{2,6},{3,7},{4,0},{5,1},{6,2},{7,3},{8,12},{9,13},{10,... | collective-permute-start | bytes 196616 | tf_op jit(solution)/shard_map/ppermute | solution.py:441
  48.5 0.0 collective-permute-start.4
  48.5 0.0 collective-permute-done.refs_1_
  48.5 3.6 %collective-permute-start.5 = (bf16[8,32,128]{2,1,0:T(8,128)(2,1)S(1)}, bf16[8,32,128]{2,1,0:T(8,128)(2,1)S(1)}, u32[]{:S(2)}, u32[]{:S(2)}) collective-permute-start(bf16[8,32,128]{2,1,0:T(8,128)(2,1)S(1)} %get-tuple-element.36), channel_id=1, source_target_pairs={{0,6},{1,7},{2,4},{3,5},{4,2},{5,3},{6,0},{7,1},{8,14},{9,15},{10,... | collective-permute-start | bytes 196616 | tf_op jit(solution)/shard_map/ppermute | solution.py:441
  52.1 3.0 %collective-permute-done.1.refs_2_ = bf16[8,32,128]{2,1,0:T(8,128)(2,1)S(1)} collective-permute-done((bf16[8,32,128]{2,1,0:T(8,128)(2,1)S(1)}, bf16[8,32,128]{2,1,0:T(8,128)(2,1)S(1)}, u32[]{:S(2)}, u32[]{:S(2)}) %collective-permute-start.1) | collective-permute-done | bytes 65568 | tf_op jit(solution)/shard_map/ppermute | solution.py:441
  55.1 0.0 copy-start.7
  55.1 2.0 %collective-permute-start.6 = (bf16[8,32,128]{2,1,0:T(8,128)(2,1)S(1)}, bf16[8,32,128]{2,1,0:T(8,128)(2,1)S(1)}, u32[]{:S(2)}, u32[]{:S(2)}) collective-permute-start(bf16[8,32,128]{2,1,0:T(8,128)(2,1)S(1)} %get-tuple-element.37), channel_id=1, source_target_pairs={{0,7},{1,6},{2,5},{3,4},{4,3},{5,2},{6,1},{7,0},{8,15},{9,14},{10,... | collective-permute-start | bytes 196616 | tf_op jit(solution)/shard_map/ppermute | solution.py:441
  57.1 0.0 copy-done.7
  57.1 0.0 collective-permute-done.2.refs_3_
  57.2 9.3 %collective-permute-done.3.refs_4_ = bf16[8,32,128]{2,1,0:T(8,128)(2,1)S(1)} collective-permute-done((bf16[8,32,128]{2,1,0:T(8,128)(2,1)S(1)}, bf16[8,32,128]{2,1,0:T(8,128)(2,1)S(1)}, u32[]{:S(2)}, u32[]{:S(2)}) %collective-permute-start.3) | collective-permute-done | bytes 65568 | tf_op jit(solution)/shard_map/ppermute | solution.py:441
  66.5 0.3 collective-permute-done.4.refs_5_
  66.7 0.0 collective-permute-done.5.refs_6_
  66.7 0.0 collective-permute-done.6.refs_7_
  66.7 0.0 all-to-all-done.1
  66.7 0.0 copy-done.4
  66.8 0.0 copy-done.5
  66.8 3.5 %middle.1 = (f32[8,256,128]{2,1,0:T(8,128)S(1)}, bf16[8,256,128]{2,1,0:T(8,128)(2,1)S(1)}, bf16[16,4,8,256]{3,2,1,0:T(8,128)(2,1)S(1)}) custom-call(bf16[1024,256]{1,0:T(8,128)(2,1)S(1)} %bitcast.4, bf16[128,128]{1,0:T(8,128)(2,1)S(1)} %copy-done.4, bf16[128,128]{1,0:T(8,128)(2,1)S(1)} %copy-done.5, bf16[8,128]{1,0:T(8,128)(2,1)S(1)} %pad.4.bias_ref, ...), custom_call_target="tpu_custom_call" | custom-call | tf_op jit(solution)/shard_map/middle/pallas_call | solution.py:266
  70.3 0.0 copy-start.6
  70.3 17.7 %all_to_all.16.ba_ref = bf16[16,4,8,256]{3,2,1,0:T(8,128)(2,1)S(1)} all-to-all(bf16[16,4,8,256]{3,2,1,0:T(8,128)(2,1)S(1)} %get-tuple-element.44), channel_id=1, replica_groups=mesh['row'=4,'z'=4,'core'=2] {'row','z'}, dimensions={0} | all-to-all | bytes 524288 | tf_op jit(solution)/shard_map/all_to_all | solution.py:451
  88.0 0.0 collective-permute-start.7
  88.0 0.0 copy-done.6
  88.0 0.0 copy-start.3
  88.0 0.7 project.1
  88.8 0.8 collective-permute-done.7.bb_ref
  89.6 0.0 copy-done.3
  89.6 0.0 copy-start.1
  89.6 4.9 %attention.1 = (bf16[8,32,128]{2,1,0:T(8,128)(2,1)S(1)}, bf16[8,32,128]{2,1,0:T(8,128)(2,1)S(1)}, bf16[8,32,128]{2,1,0:T(8,128)(2,1)S(1)}, bf16[8,32,128]{2,1,0:...) custom-call(s32[1]{0:T(128)S(6)} %copy.9.valid_ref, ...), custom_call_target="tpu_custom_call" | custom-call | tf_op jit(solution)/shard_map/attention/pallas_call | solution.py:309
  94.5 0.2 collective-permute-start.8
  94.7 0.1 collective-permute-start.9
  94.8 1.7 %collective-permute-start.10 = (bf16[8,32,128]{2,1,0:T(8,128)(2,1)S(1)}, bf16[8,32,128]{2,1,0:T(8,128)(2,1)S(1)}, u32[]{:S(2)}, u32[]{:S(2)}) collective-permute-start(bf16[8,32,128]{2,1,0:T(8,128)(2,1)S(1)} %get-tuple-element.48), channel_id=1, source_target_pairs={{0,3},{1,2},{2,1},{3,0},{4,7},{5,6},{6,5},{7,4},{8,11},{9,10},{10,... | collective-permute-start | bytes 196616 | tf_op jit(solution)/shard_map/ppermute | solution.py:326
  96.4 0.0 collective-permute-start.11
  96.5 2.7 %collective-permute-start.12 = (bf16[8,32,128]{2,1,0:T(8,128)(2,1)S(1)}, bf16[8,32,128]{2,1,0:T(8,128)(2,1)S(1)}, u32[]{:S(2)}, u32[]{:S(2)}) collective-permute-start(bf16[8,32,128]{2,1,0:T(8,128)(2,1)S(1)} %get-tuple-element.50), channel_id=1, source_target_pairs={{0,5},{1,4},{2,7},{3,6},{4,1},{5,0},{6,3},{7,2},{8,13},{9,12},{10,... | collective-permute-start | bytes 196616 | tf_op jit(solution)/shard_map/ppermute | solution.py:326
  99.1 0.0 collective-permute-done.8.refs_1_
  99.1 0.0 collective-permute-start.13
  99.1 0.6 collective-permute-done.9.refs_2_
  99.7 3.0 %collective-permute-start.14 = (bf16[8,32,128]{2,1,0:T(8,128)(2,1)S(1)}, bf16[8,32,128]{2,1,0:T(8,128)(2,1)S(1)}, u32[]{:S(2)}, u32[]{:S(2)}) collective-permute-start(bf16[8,32,128]{2,1,0:T(8,128)(2,1)S(1)} %get-tuple-element.52), channel_id=1, source_target_pairs={{0,7},{1,6},{2,5},{3,4},{4,3},{5,2},{6,1},{7,0},{8,15},{9,14},{10,... | collective-permute-start | bytes 196616 | tf_op jit(solution)/shard_map/ppermute | solution.py:326
  102.6 0.0 collective-permute-done.10.refs_3_
  102.6 4.3 %collective-permute-done.11.refs_4_ = bf16[8,32,128]{2,1,0:T(8,128)(2,1)S(1)} collective-permute-done((bf16[8,32,128]{2,1,0:T(8,128)(2,1)S(1)}, bf16[8,32,128]{2,1,0:T(8,128)(2,1)S(1)}, u32[]{:S(2)}, u32[]{:S(2)}) %collective-permute-start.11) | collective-permute-done | bytes 65568 | tf_op jit(solution)/shard_map/ppermute | solution.py:326
  106.9 1.3 %collective-permute-done.12.refs_5_ = bf16[8,32,128]{2,1,0:T(8,128)(2,1)S(1)} collective-permute-done((bf16[8,32,128]{2,1,0:T(8,128)(2,1)S(1)}, bf16[8,32,128]{2,1,0:T(8,128)(2,1)S(1)}, u32[]{:S(2)}, u32[]{:S(2)}) %collective-permute-start.12) | collective-permute-done | bytes 65568 | tf_op jit(solution)/shard_map/ppermute | solution.py:326
  108.2 0.0 collective-permute-done.13.refs_6_
  108.2 0.0 collective-permute-done.14.refs_7_
  108.2 0.0 copy-done.1
  108.2 1.1 add.3
  (1 shorter events, 0.0 us)
Async XLA Ops:
  0.7 1.2 %copy-start = (f32[64,32,128]{2,1,0:T(8,128)S(1)}, f32[64,32,128]{2,1,0:T(8,128)}, u32[]{:S(2)}) copy-start(f32[64,32,128]{2,1,0:T(8,128)} %x_ref.3) | copy-start | bytes 3145732
  1.9 0.9 copy-start.2
  41.2 25.6 %copy-start.4 = (bf16[128,128]{1,0:T(8,128)(2,1)S(1)}, bf16[128,128]{1,0:T(8,128)(2,1)}, u32[]{:S(2)}) copy-start(bf16[128,128]{1,0:T(8,128)(2,1)} %gate_ref.1) | copy-start | bytes 98308
  41.2 25.6 %copy-start.5 = (bf16[128,128]{1,0:T(8,128)(2,1)S(1)}, bf16[128,128]{1,0:T(8,128)(2,1)}, u32[]{:S(2)}) copy-start(bf16[128,128]{1,0:T(8,128)(2,1)} %tri_ref.3) | copy-start | bytes 98308
  41.2 25.6 %all-to-all-start.1 = ((bf16[32,32,256]{2,1,0:T(8,128)(2,1)}), bf16[32,32,256]{2,1,0:T(8,128)(2,1)S(1)}, u32[]{:S(2)}, u32[]{:S(2)}) async-start(bf16[32,32,256]{2,1,0:T(8,128)(2,1)} %bitcast.1), calls=%async_computation.1 | async-start | bytes 1048576 | tf_op jit(solution)/shard_map/all_to_all | solution.py:448
  43.9 4.6 %collective-permute-start = (bf16[8,32,128]{2,1,0:T(8,128)(2,1)S(1)}, bf16[8,32,128]{2,1,0:T(8,128)(2,1)S(1)}, u32[]{:S(2)}, u32[]{:S(2)}) collective-permute-start(bf16[8,32,128]{2,1,0:T(8,128)(2,1)S(1)} %get-tuple-element.31), channel_id=1, source_target_pairs={{0,1},{1,0},{2,3},{3,2},{4,5},{5,4},{6,7},{7,6},{8,9},{9,8},{10,11... | collective-permute-start | bytes 196616 | tf_op jit(solution)/shard_map/ppermute | solution.py:441
  44.1 11.0 %collective-permute-start.1 = (bf16[8,32,128]{2,1,0:T(8,128)(2,1)S(1)}, bf16[8,32,128]{2,1,0:T(8,128)(2,1)S(1)}, u32[]{:S(2)}, u32[]{:S(2)}) collective-permute-start(bf16[8,32,128]{2,1,0:T(8,128)(2,1)S(1)} %get-tuple-element.32), channel_id=1, source_target_pairs={{0,2},{1,3},{2,0},{3,1},{4,6},{5,7},{6,4},{7,5},{8,10},{9,11},{10,... | collective-permute-start | bytes 196616 | tf_op jit(solution)/shard_map/ppermute | solution.py:441
  45.8 11.3 %collective-permute-start.2 = (bf16[8,32,128]{2,1,0:T(8,128)(2,1)S(1)}, bf16[8,32,128]{2,1,0:T(8,128)(2,1)S(1)}, u32[]{:S(2)}, u32[]{:S(2)}) collective-permute-start(bf16[8,32,128]{2,1,0:T(8,128)(2,1)S(1)} %get-tuple-element.33), channel_id=1, source_target_pairs={{0,3},{1,2},{2,1},{3,0},{4,7},{5,6},{6,5},{7,4},{8,11},{9,10},{10,... | collective-permute-start | bytes 196616 | tf_op jit(solution)/shard_map/ppermute | solution.py:441
  45.8 20.6 %collective-permute-start.3 = (bf16[8,32,128]{2,1,0:T(8,128)(2,1)S(1)}, bf16[8,32,128]{2,1,0:T(8,128)(2,1)S(1)}, u32[]{:S(2)}, u32[]{:S(2)}) collective-permute-start(bf16[8,32,128]{2,1,0:T(8,128)(2,1)S(1)} %get-tuple-element.34), channel_id=1, source_target_pairs={{0,4},{1,5},{2,6},{3,7},{4,0},{5,1},{6,2},{7,3},{8,12},{9,13},{10,... | collective-permute-start | bytes 196616 | tf_op jit(solution)/shard_map/ppermute | solution.py:441
  48.5 18.2 %collective-permute-start.4 = (bf16[8,32,128]{2,1,0:T(8,128)(2,1)S(1)}, bf16[8,32,128]{2,1,0:T(8,128)(2,1)S(1)}, u32[]{:S(2)}, u32[]{:S(2)}) collective-permute-start(bf16[8,32,128]{2,1,0:T(8,128)(2,1)S(1)} %get-tuple-element.35), channel_id=1, source_target_pairs={{0,5},{1,4},{2,7},{3,6},{4,1},{5,0},{6,3},{7,2},{8,13},{9,12},{10,... | collective-permute-start | bytes 196616 | tf_op jit(solution)/shard_map/ppermute | solution.py:441
  48.5 18.2 %collective-permute-start.5 = (bf16[8,32,128]{2,1,0:T(8,128)(2,1)S(1)}, bf16[8,32,128]{2,1,0:T(8,128)(2,1)S(1)}, u32[]{:S(2)}, u32[]{:S(2)}) collective-permute-start(bf16[8,32,128]{2,1,0:T(8,128)(2,1)S(1)} %get-tuple-element.36), channel_id=1, source_target_pairs={{0,6},{1,7},{2,4},{3,5},{4,2},{5,3},{6,0},{7,1},{8,14},{9,15},{10,... | collective-permute-start | bytes 196616 | tf_op jit(solution)/shard_map/ppermute | solution.py:441
  55.1 2.0 %copy-start.7 = (bf16[128,4]{0,1:T(4,128)(2,1)S(1)}, bf16[128,4]{0,1:T(4,128)(2,1)}, u32[]{:S(2)}) copy-start(bf16[128,4]{0,1:T(4,128)(2,1)} %param.14) | copy-start | bytes 3076
  55.1 11.6 %collective-permute-start.6 = (bf16[8,32,128]{2,1,0:T(8,128)(2,1)S(1)}, bf16[8,32,128]{2,1,0:T(8,128)(2,1)S(1)}, u32[]{:S(2)}, u32[]{:S(2)}) collective-permute-start(bf16[8,32,128]{2,1,0:T(8,128)(2,1)S(1)} %get-tuple-element.37), channel_id=1, source_target_pairs={{0,7},{1,6},{2,5},{3,4},{4,3},{5,2},{6,1},{7,0},{8,15},{9,14},{10,... | collective-permute-start | bytes 196616 | tf_op jit(solution)/shard_map/ppermute | solution.py:441
  70.3 17.8 %copy-start.6 = (bf16[128,512]{1,0:T(8,128)(2,1)S(1)}, bf16[128,512]{1,0:T(8,128)(2,1)}, u32[]{:S(2)}) copy-start(bf16[128,512]{1,0:T(8,128)(2,1)} %w_ref.1) | copy-start | bytes 393220
  88.0 1.5 %collective-permute-start.7 = (bf16[16,4,8,256]{3,2,1,0:T(8,128)(2,1)S(1)}, bf16[16,4,8,256]{3,2,1,0:T(8,128)(2,1)S(1)}, u32[]{:S(2)}, u32[]{:S(2)}) collective-permute-start(bf16[16,4,8,256]{3,2,1,0:T(8,128)(2,1)S(1)} %all_to_all.16.ba_ref), channel_id=1, source_target_pairs={{0,1},{1,0},{2,3},{3,2},{4,5},{5,4},{6,7},{7,6},{8,9},{9,8},{10,11... | collective-permute-start | bytes 786440 | tf_op jit(solution)/shard_map/ppermute | solution.py:452
  88.0 1.5 %copy-start.3 = (bf16[128,128]{1,0:T(8,128)(2,1)S(1)}, bf16[128,128]{1,0:T(8,128)(2,1)}, u32[]{:S(2)}) copy-start(bf16[128,128]{1,0:T(8,128)(2,1)} %wo_ref.1) | copy-start | bytes 98308
  89.6 18.6 %copy-start.1 = (f32[64,32,128]{2,1,0:T(8,128)S(1)}, f32[64,32,128]{2,1,0:T(8,128)}, u32[]{:S(2)}) copy-start(f32[64,32,128]{2,1,0:T(8,128)} %x_ref.3) | copy-start | bytes 3145732
  94.5 4.6 %collective-permute-start.8 = (bf16[8,32,128]{2,1,0:T(8,128)(2,1)S(1)}, bf16[8,32,128]{2,1,0:T(8,128)(2,1)S(1)}, u32[]{:S(2)}, u32[]{:S(2)}) collective-permute-start(bf16[8,32,128]{2,1,0:T(8,128)(2,1)S(1)} %get-tuple-element.46), channel_id=1, source_target_pairs={{0,1},{1,0},{2,3},{3,2},{4,5},{5,4},{6,7},{7,6},{8,9},{9,8},{10,11... | collective-permute-start | bytes 196616 | tf_op jit(solution)/shard_map/ppermute | solution.py:326
  94.7 5.0 %collective-permute-start.9 = (bf16[8,32,128]{2,1,0:T(8,128)(2,1)S(1)}, bf16[8,32,128]{2,1,0:T(8,128)(2,1)S(1)}, u32[]{:S(2)}, u32[]{:S(2)}) collective-permute-start(bf16[8,32,128]{2,1,0:T(8,128)(2,1)S(1)} %get-tuple-element.47), channel_id=1, source_target_pairs={{0,2},{1,3},{2,0},{3,1},{4,6},{5,7},{6,4},{7,5},{8,10},{9,11},{10,... | collective-permute-start | bytes 196616 | tf_op jit(solution)/shard_map/ppermute | solution.py:326
  94.8 7.9 %collective-permute-start.10 = (bf16[8,32,128]{2,1,0:T(8,128)(2,1)S(1)}, bf16[8,32,128]{2,1,0:T(8,128)(2,1)S(1)}, u32[]{:S(2)}, u32[]{:S(2)}) collective-permute-start(bf16[8,32,128]{2,1,0:T(8,128)(2,1)S(1)} %get-tuple-element.48), channel_id=1, source_target_pairs={{0,3},{1,2},{2,1},{3,0},{4,7},{5,6},{6,5},{7,4},{8,11},{9,10},{10,... | collective-permute-start | bytes 196616 | tf_op jit(solution)/shard_map/ppermute | solution.py:326
  96.4 10.5 %collective-permute-start.11 = (bf16[8,32,128]{2,1,0:T(8,128)(2,1)S(1)}, bf16[8,32,128]{2,1,0:T(8,128)(2,1)S(1)}, u32[]{:S(2)}, u32[]{:S(2)}) collective-permute-start(bf16[8,32,128]{2,1,0:T(8,128)(2,1)S(1)} %get-tuple-element.49), channel_id=1, source_target_pairs={{0,4},{1,5},{2,6},{3,7},{4,0},{5,1},{6,2},{7,3},{8,12},{9,13},{10,... | collective-permute-start | bytes 196616 | tf_op jit(solution)/shard_map/ppermute | solution.py:326
  96.5 11.8 %collective-permute-start.12 = (bf16[8,32,128]{2,1,0:T(8,128)(2,1)S(1)}, bf16[8,32,128]{2,1,0:T(8,128)(2,1)S(1)}, u32[]{:S(2)}, u32[]{:S(2)}) collective-permute-start(bf16[8,32,128]{2,1,0:T(8,128)(2,1)S(1)} %get-tuple-element.50), channel_id=1, source_target_pairs={{0,5},{1,4},{2,7},{3,6},{4,1},{5,0},{6,3},{7,2},{8,13},{9,12},{10,... | collective-permute-start | bytes 196616 | tf_op jit(solution)/shard_map/ppermute | solution.py:326
  99.1 9.1 %collective-permute-start.13 = (bf16[8,32,128]{2,1,0:T(8,128)(2,1)S(1)}, bf16[8,32,128]{2,1,0:T(8,128)(2,1)S(1)}, u32[]{:S(2)}, u32[]{:S(2)}) collective-permute-start(bf16[8,32,128]{2,1,0:T(8,128)(2,1)S(1)} %get-tuple-element.51), channel_id=1, source_target_pairs={{0,6},{1,7},{2,4},{3,5},{4,2},{5,3},{6,0},{7,1},{8,14},{9,15},{10,... | collective-permute-start | bytes 196616 | tf_op jit(solution)/shard_map/ppermute | solution.py:326
  99.7 8.5 %collective-permute-start.14 = (bf16[8,32,128]{2,1,0:T(8,128)(2,1)S(1)}, bf16[8,32,128]{2,1,0:T(8,128)(2,1)S(1)}, u32[]{:S(2)}, u32[]{:S(2)}) collective-permute-start(bf16[8,32,128]{2,1,0:T(8,128)(2,1)S(1)} %get-tuple-element.52), channel_id=1, source_target_pairs={{0,7},{1,6},{2,5},{3,4},{4,3},{5,2},{6,1},{7,0},{8,15},{9,14},{10,... | collective-permute-start | bytes 196616 | tf_op jit(solution)/shard_map/ppermute | solution.py:326
